TPU v7x, 1024 devices: a whole 4x4x32 slice. The times are simulated.
1024 devices in a mesh: gx: 32 (over z), gy: 8 (over y, core), gz: 4 (over x).
Axes of the slice: x: 4, y: 4, z: 32, core: 2. Of those that a mesh axis runs over, the one named last changes fastest.
Arguments:
- coarse_source: float32 [512, 256, 512], P('gx', 'gy', 'gz'), may hold values from -6 to 6
- coarse_shift: float32 [512, 256, 512], P('gx', 'gy', 'gz'), may hold values from 0.1 to 4
- coarse_start: float32 [512, 256, 512], P('gx', 'gy', 'gz'), may hold values from -3 to 3
- fine_source: float32 [4096, 32768], P(('gx', 'gy', 'gz')), may hold values from -6 to 6
- fine_shift: float32 [4096, 32768], P(('gx', 'gy', 'gz')), may hold values from 0.1 to 4
- fine_start: float32 [4096, 32768], P(('gx', 'gy', 'gz')), may hold values from -3 to 3
- box_corner: int32 [1024, 4, 3], P(('gx', 'gy', 'gz')), may hold values from 0 to 992, as said below
- box_owner: int32 [1024, 4], P(('gx', 'gy', 'gz')), may hold values from 0 to 32, as said below
Outputs:
- potential: float32 [512, 256, 512], P('gx', 'gy', 'gz')
- fine_solution: float32 [4096, 32768], P(('gx', 'gy', 'gz'))
- residual_norms: float32 [2], replicated
Inputs may be any that keep to these rules, and one draw needn't show every extreme that they name: `box_owner`: each device has at least one live slot; in every group of 32 devices that share a gx index some device has 4 live slots; the live owners of one device are distinct; no device is the owner of more than 4 live boxes, and in every group some device is the owner of exactly 4 live boxes. `box_corner`: each corner is a multiple of 32 and its footprint lies in the coarse block of the device that lists it; the 4 footprints of one device are distinct.
All inputs are finite; a program needn't handle non-finite values.
Results may differ from a plain program's by a relative error of at most 0.0001.
Values sent between devices are 32-bit elements; how exact they have to be, the bound alone decides.
A program may use at most 128 MiB of HBM per device.

v0:
```python
import functools

import jax
import jax.numpy as jnp
from jax import lax
from jax.sharding import Mesh
from jax.sharding import PartitionSpec as P

FOOT = 16
CYCLES = 2
CSWEEPS = 4
FSWEEPS = 3
GY = ("gy_0", "gy_1")
GY_GZ = ("gy_0", "gy_1", "gz")
GX_GY_GZ = ("gx", "gy_0", "gy_1", "gz")


OMEGA = 0.8
HIGHEST = lax.Precision.HIGHEST


def sent_together(arrays, axis, split_dim, concat_dim, along):
    ends, at = ([], 0)
    for a in arrays[:-1]:
        at += a.shape[along]
        ends.append(at)
    both = jnp.concatenate(arrays, axis=along)
    return tuple(
        jnp.split(
            lax.all_to_all(both, axis, split_axis=split_dim, concat_axis=concat_dim, tiled=True),
            ends,
            axis=along,
        )
    )


def with_halo(array, sides, width):
    edges = {}
    for axis, dim in sides:
        devices, length = (lax.axis_size(axis), array.shape[dim])
        up = [(i, (i + 1) % devices) for i in range(devices - 1)]
        last = lax.slice_in_dim(array, length - width, length, axis=dim)
        initial = lax.slice_in_dim(array, 0, width, axis=dim)
        edges[dim] = (
            lax.ppermute(last, axis, up),
            lax.ppermute(initial, axis, [(b, a) for a, b in up]),
        )
    done = []
    for _, dim in sides:
        low, high = edges[dim]
        around = [(width, width) if d in done else (0, 0) for d in range(array.ndim)]
        array = jnp.concatenate([jnp.pad(low, around), array, jnp.pad(high, around)], axis=dim)
        done.append(dim)
    return array


def by_axis(array, axes):
    return functools.reduce(lax.psum, axes, array)


def to_blocks(field):
    extent = field.shape
    shaped = field.reshape(
        extent[0] // FOOT, FOOT, extent[1] // FOOT, FOOT, extent[2] // FOOT, FOOT
    )
    return shaped.transpose(0, 2, 4, 1, 3, 5).reshape(-1, FOOT * FOOT * FOOT)


def from_blocks(blocks, extent):
    shaped = blocks.reshape(
        extent[0] // FOOT, extent[1] // FOOT, extent[2] // FOOT, FOOT, FOOT, FOOT
    )
    return shaped.transpose(0, 3, 1, 4, 2, 5).reshape(extent)


def inject(parents):
    number = parents.shape[0]
    shaped = parents.reshape(number, FOOT, 1, FOOT, 1, FOOT, 1)
    spread = jnp.broadcast_to(shaped, (number, FOOT, 2, FOOT, 2, FOOT, 2))
    return spread.reshape(number, 8 * FOOT * FOOT * FOOT)


def restrict(values):
    number = values.shape[0]
    return (
        values.reshape(number, FOOT, 2, FOOT, 2, FOOT, 2)
        .mean(axis=(2, 4, 6))
        .reshape(number, FOOT * FOOT * FOOT)
    )


def fine_residual(values, parents, source, shift):
    ghost = inject(parents)
    side = 2 * FOOT
    position = jnp.arange(side * side * side, dtype=jnp.int32)[None, :]
    summed = jnp.zeros_like(values)
    for stride in (1, side, side * side):
        coordinate = position // stride % side
        upper = jnp.roll(values, -stride, axis=1)
        lower = jnp.roll(values, stride, axis=1)
        summed = (
            summed
            + jnp.where(coordinate < side - 1, upper, ghost)
            + jnp.where(coordinate > 0, lower, ghost)
        )
    return source - (6.0 + shift) * values + summed


def beside_sum(padded):
    summed = padded[2:, 1:-1, 1:-1] + padded[:-2, 1:-1, 1:-1]
    summed = summed + padded[1:-1, 2:, 1:-1] + padded[1:-1, :-2, 1:-1]
    return summed + padded[1:-1, 1:-1, 2:] + padded[1:-1, 1:-1, :-2]


def local(
    coarse_source,
    coarse_shift,
    coarse_start,
    fine_source,
    fine_shift,
    fine_start,
    box_corner,
    box_owner,
):
    extent = coarse_source.shape
    size_y = lax.axis_size(GY)
    size_z = lax.axis_size("gz")
    group = size_y * size_z
    slots = box_owner.shape[1]
    anchor = jnp.stack(
        [
            lax.axis_index("gx") * extent[0],
            lax.axis_index(GY) * extent[1],
            lax.axis_index("gz") * extent[2],
        ]
    )
    along_y = extent[1] // FOOT
    along_z = extent[2] // FOOT
    places = extent[0] // FOOT * along_y * along_z
    block = (box_corner[0] // 2 - anchor[None, :]) // FOOT
    location = (block[:, 0] * along_y + block[:, 1]) * along_z + block[:, 2]
    live = (box_owner[0] < group).astype(jnp.float32)
    peer_ids = jnp.arange(group, dtype=jnp.int32)
    route = (box_owner[0][None, :] == peer_ids[:, None]).astype(jnp.float32) * live[None, :]
    locate = (jnp.arange(places, dtype=jnp.int32)[:, None] == location[None, :]).astype(jnp.float32)
    collect = jnp.dot(route, locate.T, precision=HIGHEST)
    deposit = collect.T
    live_out = jnp.sum(route, axis=1, keepdims=True)
    diagonal = 6.0 + coarse_shift
    fine_diagonal = 6.0 + fine_shift

    def send_parents(potential):
        outgoing = jnp.dot(collect, to_blocks(potential), precision=HIGHEST)
        parents, flags = sent_together((outgoing, live_out), GY_GZ, 0, 0, 1)
        return (parents, flags)

    potential = coarse_start
    values = fine_start
    earlier = None
    norms = []
    pick = None
    occupied = None
    for cycle in range(CYCLES):
        received, flags = send_parents(potential)
        if pick is None:
            flag_vec = flags[:, 0]
            before = jnp.cumsum(flag_vec) - flag_vec
            pick = (jnp.arange(slots, dtype=jnp.float32)[:, None] == before[None, :]).astype(
                jnp.float32
            ) * flag_vec[None, :]
            occupied = jnp.sum(pick, axis=1, keepdims=True)
        parents = jnp.dot(pick, received, precision=HIGHEST)
        if cycle > 0:
            values = values + inject(parents - earlier)
        for sweep in range(FSWEEPS):
            values = (
                values
                + OMEGA * fine_residual(values, parents, fine_source, fine_shift) / fine_diagonal
            )
        remainder = fine_residual(values, parents, fine_source, fine_shift)
        sent_back = jnp.dot(pick.T, restrict(remainder) * occupied, precision=HIGHEST)
        returned = lax.all_to_all(sent_back, GY_GZ, split_axis=0, concat_axis=0, tiled=True)
        composite = coarse_source + from_blocks(
            jnp.dot(deposit, returned, precision=HIGHEST), extent
        )
        smooth_potential = potential
        for smooth_sweep in range(CSWEEPS):
            padded = with_halo(smooth_potential, (("gx", 0), (GY, 1), ("gz", 2)), 1)
            residual = composite - diagonal * smooth_potential + beside_sum(padded)
            smooth_potential = smooth_potential + OMEGA * residual / diagonal
        potential = smooth_potential
        squares = jnp.sum(residual * residual)
        local_sum = squares + jnp.sum(occupied * remainder * remainder)
        norms.append(by_axis(local_sum, GX_GY_GZ))
        earlier = parents
    received, flags = send_parents(potential)
    parents = jnp.dot(pick, received, precision=HIGHEST)
    values = (values + inject(parents - earlier)) * occupied
    cells = float(extent[0] * extent[1] * extent[2] * lax.axis_size("gx") * size_y * size_z)
    return (potential, values, jnp.sqrt(jnp.stack(norms) / cells))


def solution(mesh):
    split = Mesh(
        mesh.devices.reshape(mesh.shape["gx"], 4, 2, mesh.shape["gz"]), ("gx", "gy_0", "gy_1", "gz")
    )
    return jax.shard_map(
        local,
        mesh=split,
        in_specs=(
            P("gx", GY, "gz"),
            P("gx", GY, "gz"),
            P("gx", GY, "gz"),
            P(GX_GY_GZ, None),
            P(GX_GY_GZ, None),
            P(GX_GY_GZ, None),
            P(GX_GY_GZ, None, None),
            P(GX_GY_GZ, None),
        ),
        out_specs=(P("gx", GY, "gz"), P(GX_GY_GZ, None), P()),
        check_vma=False,
    )
```

profile of v0, /device:TPU:1, one launch (start us, length us, event | category | flops | bytes accessed | tf_op | source)
XLA Modules:
  0.0 589.2 jit_solution(6615624938966737031)
XLA Ops:
  2.1 16.0 %collective-permute-start.2 = (f32[16,1,128]{2,1,0:T(1,128)}, f32[16,1,128]{2,1,0:T(1,128)}, u32[]{:S(2)}, u32[]{:S(2)}) collective-permute-start(f32[16,1,128]{2,1,0:T(1,128)} %get-tuple-element.174), channel_id=1, source_target_pairs={{4,0},{8,4},{12,8},{16,12},{20,16},{24,20},{28,24},{5,1},{9,5},{13... | collective-permute-start | bytes 24584 | tf_op jit(solution)/shard_map/ppermute | solution.py:46
  31.5 4.9 all-to-all-start
  40.2 7.8 %all-to-all-done = f32[32,1,4097]{2,1,0:T(1,128)S(1)} async-done(((f32[32,1,4097]{2,1,0:T(1,128)}), f32[32,1,4097]{2,1,0:T(1,128)S(1)}, u32[]{:S(2)}, u32[]{:S(2)}) %all-to-all-start) | async-done | bytes 524448 | tf_op jit(solution)/shard_map/all_to_all | solution.py:30
  49.3 9.5 %broadcast_in_dim.311 = f32[4,16,2,16,2,16,2]{0,6,5,4,3,2,1:T(2,128)} broadcast(f32[4,16,16,16]{0,3,2,1:T(8,128)S(1)} %bitcast.130), dimensions={0,1,3,5} | broadcast | bytes 589824 | tf_op jit(solution)/shard_map/broadcast_in_dim | solution.py:79
  58.8 9.6 %copy.404 = f32[4,32768]{1,0:T(4,128)S(1)} copy(f32[4,32768]{0,1:T(8,128)} %bitcast.122) | data formatting | bytes 1048576 | tf_op jit(solution)/shard_map/reshape | solution.py:80
  68.4 3.9 fusion.75
  83.1 8.5 %copy.428 = f32[4,32768]{0,1:T(8,128)} copy(f32[4,32768]{1,0:T(4,128)S(1)} %fusion.39) | data formatting | bytes 1048576 | tf_op jit(solution)/shard_map/add | solution.py:106
  91.5 14.1 %reduce_sum.77 = f32[4,16,16,16]{0,3,2,1:T(8,128)} reduce(f32[4,16,2,16,2,16,2]{0,6,5,4,3,2,1:T(2,128)} %bitcast.127, f32[]{:T(128)} %constant.222.clone.1), dimensions={2,4,6}, to_apply=%region_2.3 | reduce | flops 114688 | bytes 589828 | tf_op jit(solution)/shard_map/reduce_sum | solution.py:87
  110.7 4.3 all-to-all-start.1
  115.9 3.9 collective-permute-start.5
  128.2 16.3 %convolution_bitcast_fusion.3 = f32[1,16,2,16,8,16]{5,4,3,1,2,0:T(8,128)S(1)} fusion(f32[16,16,16,32,1]{3,2,1,0,4:T(8,128)} %bitcast.132, f32[32,16]{0,1:T(8,128)S(1)} %fusion.171), kind=kOutput, calls=%fused_computation.9 | convolution fusion | flops 25165824 | bytes 788480 | tf_op jit(solution)/shard_map/dot_general | solution.py:184
  156.6 4.0 collective-permute-start.7
  164.8 4.6 collective-permute-done.11
  169.4 3.9 collective-permute-done.10
  180.7 4.0 collective-permute-start.13
  188.8 4.3 collective-permute-done.17
  193.1 3.9 collective-permute-done.16
  201.7 4.0 collective-permute-start.19
  214.1 4.1 collective-permute-done.23
  218.2 4.2 collective-permute-done.22
  233.0 15.6 %all_to_all.60 = f32[32,1,4097]{2,1,0:T(1,128)S(1)} all-to-all(f32[32,1,4097]{2,1,0:T(1,128)S(1)} %copy.434), channel_id=1, replica_groups=mesh['gx'=32,'gy_0'=4,'gy_1'=2,'gz'=4] {'gy_0','gy_1','gz'}, dimensions={0} | all-to-all | bytes 1048832 | tf_op jit(solution)/shard_map/all_to_all | solution.py:30
  251.0 10.4 %broadcast_in_dim.318 = f32[4,16,2,16,2,16,2]{0,6,5,4,3,2,1:T(2,128)} broadcast(f32[4,16,16,16]{0,3,2,1:T(8,128)} %bitcast.128), dimensions={0,1,3,5} | broadcast | bytes 589824 | tf_op jit(solution)/shard_map/broadcast_in_dim | solution.py:79
  261.4 9.5 %copy.436 = f32[4,32768]{1,0:T(4,128)S(1)} copy(f32[4,32768]{0,1:T(8,128)} %bitcast.123) | data formatting | bytes 1048576 | tf_op jit(solution)/shard_map/reshape | solution.py:80
  276.5 10.4 %broadcast_in_dim.320 = f32[4,16,2,16,2,16,2]{0,6,5,4,3,2,1:T(2,128)} broadcast(f32[4,16,16,16]{0,3,2,1:T(8,128)} %bitcast.131), dimensions={0,1,3,5} | broadcast | bytes 589824 | tf_op jit(solution)/shard_map/broadcast_in_dim | solution.py:79
  286.9 9.5 %copy.438 = f32[4,32768]{1,0:T(4,128)S(1)} copy(f32[4,32768]{0,1:T(8,128)} %bitcast.124) | data formatting | bytes 1048576 | tf_op jit(solution)/shard_map/reshape | solution.py:80
  296.4 3.9 fusion.72
  308.6 4.0 fusion.3
  312.6 9.4 %copy.462 = f32[4,32768]{0,1:T(8,128)} copy(f32[4,32768]{1,0:T(4,128)} %get-tuple-element.24) | data formatting | bytes 1048576 | tf_op jit(solution)/shard_map/add | solution.py:106
  322.0 13.7 %reduce_sum.80 = f32[4,16,16,16]{0,3,2,1:T(8,128)} reduce(f32[4,16,2,16,2,16,2]{0,6,5,4,3,2,1:T(2,128)} %bitcast.125, f32[]{:T(128)} %constant.222.clone.1), dimensions={2,4,6}, to_apply=%region_4.5 | reduce | flops 114688 | bytes 589828 | tf_op jit(solution)/shard_map/reduce_sum | solution.py:87
  340.8 4.3 all-to-all-start.3
  355.4 4.0 collective-permute-start.25
  362.5 16.3 %convolution_bitcast_fusion.2 = f32[1,16,2,16,8,16]{5,4,3,1,2,0:T(8,128)S(1)} fusion(f32[16,16,16,32,1]{3,2,1,0,4:T(8,128)} %bitcast.133, f32[32,16]{0,1:T(8,128)S(1)} %fusion.171), kind=kOutput, calls=%fused_computation.8 | convolution fusion | flops 25165824 | bytes 788480 | tf_op jit(solution)/shard_map/dot_general | solution.py:184
  389.9 4.0 collective-permute-start.31
  394.0 4.0 collective-permute-start.35
  399.4 4.7 collective-permute-done.35
  404.1 3.9 collective-permute-done.34
  415.3 4.0 collective-permute-start.37
  423.9 4.3 collective-permute-done.41
  436.8 4.3 collective-permute-start.43
  448.9 4.1 collective-permute-done.47
  453.0 4.3 collective-permute-done.46
  465.8 4.8 all-to-all-start.4
  473.1 56.7 %all-reduce.32 = (f32[]{:T(128)}, f32[]{:T(128)}) all-reduce(f32[]{:T(128)S(6)} %add.785, f32[]{:T(128)S(6)} %add.784), channel_id=1, replica_groups=mesh['gx'=32,'gy_0'=4,'gy_1'=2,'gz'=4] {'gx'}, use_global_device_ids=true, to_apply=%region_13.14 | all-reduce | flops 2 | bytes 16 | tf_op jit(solution)/shard_map/psum | solution.py:58
  529.9 8.5 %all-reduce.34 = (f32[]{:T(128)}, f32[]{:T(128)}) all-reduce(f32[]{:T(128)} %get-tuple-element.14, f32[]{:T(128)} %get-tuple-element.15), channel_id=1, replica_groups=mesh['gx'=32,'gy_0'=4,'gy_1'=2,'gz'=4] {'gy_0'}, use_global_device_ids=true, to_apply=%region_14.15 | all-reduce | flops 2 | bytes 16 | tf_op jit(solution)/shard_map/psum | solution.py:58
  538.4 18.8 %all-reduce.35 = (f32[]{:T(128)}, f32[]{:T(128)}) all-reduce(f32[]{:T(128)} %get-tuple-element.18, f32[]{:T(128)} %get-tuple-element.19), channel_id=1, replica_groups=mesh['gx'=32,'gy_0'=4,'gy_1'=2,'gz'=4] {'gy_1'}, use_global_device_ids=true, to_apply=%region_15.16 | all-reduce | flops 2 | bytes 16 | tf_op jit(solution)/shard_map/psum | solution.py:58
  557.2 9.0 %all-reduce.33 = (f32[1]{0:T(128)}, f32[1]{0:T(128)}) all-reduce(f32[1]{0:T(128)} %bitcast.47, f32[1]{0:T(128)} %bitcast.46), channel_id=1, replica_groups=mesh['gx'=32,'gy_0'=4,'gy_1'=2,'gz'=4] {'gz'}, use_global_device_ids=true, to_apply=%region_16.17 | all-reduce | flops 2 | bytes 16 | tf_op jit(solution)/shard_map/psum | solution.py:58
  569.1 9.5 %broadcast_in_dim.322 = f32[4,16,2,16,2,16,2]{0,6,5,4,3,2,1:T(2,128)} broadcast(f32[4,16,16,16]{0,3,2,1:T(8,128)S(1)} %bitcast.129), dimensions={0,1,3,5} | broadcast | bytes 589824 | tf_op jit(solution)/shard_map/broadcast_in_dim | solution.py:79
  578.6 9.5 %copy.470 = f32[4,32768]{1,0:T(4,128)S(1)} copy(f32[4,32768]{0,1:T(8,128)} %bitcast.126) | data formatting | bytes 1048576 | tf_op jit(solution)/shard_map/reshape | solution.py:80
  (270 shorter events, 183.6 us)
Async XLA Ops:
  2.1 119.0 %collective-permute-start.2 = (f32[16,1,128]{2,1,0:T(1,128)}, f32[16,1,128]{2,1,0:T(1,128)}, u32[]{:S(2)}, u32[]{:S(2)}) collective-permute-start(f32[16,1,128]{2,1,0:T(1,128)} %get-tuple-element.174), channel_id=1, source_target_pairs={{4,0},{8,4},{12,8},{16,12},{20,16},{24,20},{28,24},{5,1},{9,5},{13... | collective-permute-start | bytes 24584 | tf_op jit(solution)/shard_map/ppermute | solution.py:46
  18.9 105.0 %collective-permute-start.1 = (f32[1,32,128]{2,1,0:T(8,128)S(1)}, f32[1,32,128]{2,1,0:T(8,128)S(1)}, u32[]{:S(2)}, u32[]{:S(2)}) collective-permute-start(f32[1,32,128]{2,1,0:T(8,128)S(1)} %get-tuple-element.176), channel_id=1, source_target_pairs={{0,32},{32,64},{64,96},{96,128},{128,160},{160,192},{192,224},{224... | collective-permute-start | bytes 49160 | tf_op jit(solution)/shard_map/ppermute | solution.py:45
  20.2 103.0 %collective-permute-start.3 = (f32[16,1,128]{2,1,0:T(1,128)}, f32[16,1,128]{2,1,0:T(1,128)}, u32[]{:S(2)}, u32[]{:S(2)}) collective-permute-start(f32[16,1,128]{2,1,0:T(1,128)} %get-tuple-element.173), channel_id=1, source_target_pairs={{0,4},{4,8},{8,12},{12,16},{16,20},{20,24},{24,28},{1,5},{5,9},{9,... | collective-permute-start | bytes 24584 | tf_op jit(solution)/shard_map/ppermute | solution.py:45
  31.5 16.5 %all-to-all-start = ((f32[32,1,4097]{2,1,0:T(1,128)}), f32[32,1,4097]{2,1,0:T(1,128)S(1)}, u32[]{:S(2)}, u32[]{:S(2)}) async-start(f32[32,1,4097]{2,1,0:T(1,128)} %copy.402), calls=%async_computation | async-start | bytes 1081344 | tf_op jit(solution)/shard_map/all_to_all | solution.py:30
  110.7 15.8 %all-to-all-start.1 = ((f32[32,1,4096]{2,1,0:T(1,128)}), f32[32,1,4096]{2,1,0:T(1,128)S(1)}, u32[]{:S(2)}, u32[]{:S(2)}) async-start(f32[32,1,4096]{2,1,0:T(1,128)} %copy.429), calls=%async_computation.1 | async-start | bytes 1048576 | tf_op jit(solution)/shard_map/all_to_all | solution.py:182
  115.9 32.4 %collective-permute-start.5 = (f32[16,32,1]{2,1,0:T(8,128)}, f32[16,32,1]{2,1,0:T(8,128)}, u32[]{:S(2)}, u32[]{:S(2)}) collective-permute-start(f32[16,32,1]{2,1,0:T(8,128)} %get-tuple-element.172), channel_id=1, source_target_pairs={{0,1},{1,2},{2,3},{4,5},{5,6},{6,7},{8,9},{9,10},{10,11},{12,13},{... | collective-permute-start | bytes 6152 | tf_op jit(solution)/shard_map/ppermute | solution.py:45
  121.2 27.1 %collective-permute-start.4 = (f32[16,32,1]{2,1,0:T(8,128)}, f32[16,32,1]{2,1,0:T(8,128)}, u32[]{:S(2)}, u32[]{:S(2)}) collective-permute-start(f32[16,32,1]{2,1,0:T(8,128)} %get-tuple-element.171), channel_id=1, source_target_pairs={{1,0},{2,1},{3,2},{5,4},{6,5},{7,6},{9,8},{10,9},{11,10},{13,12},{... | collective-permute-start | bytes 6152 | tf_op jit(solution)/shard_map/ppermute | solution.py:46
  149.7 13.7 %collective-permute-start.8 = (f32[16,1,128]{2,1,0:T(1,128)S(1)}, f32[16,1,128]{2,1,0:T(1,128)S(1)}, u32[]{:S(2)}, u32[]{:S(2)}) collective-permute-start(f32[16,1,128]{2,1,0:T(1,128)S(1)} %get-tuple-element.170), channel_id=1, source_target_pairs={{4,0},{8,4},{12,8},{16,12},{20,16},{24,20},{28,24},{5,1},{9,5},{13... | collective-permute-start | bytes 24584 | tf_op jit(solution)/shard_map/ppermute | solution.py:46
  152.0 12.7 %collective-permute-start.9 = (f32[16,1,128]{2,1,0:T(1,128)S(1)}, f32[16,1,128]{2,1,0:T(1,128)S(1)}, u32[]{:S(2)}, u32[]{:S(2)}) collective-permute-start(f32[16,1,128]{2,1,0:T(1,128)S(1)} %get-tuple-element.169), channel_id=1, source_target_pairs={{0,4},{4,8},{8,12},{12,16},{16,20},{20,24},{24,28},{1,5},{5,9},{9,... | collective-permute-start | bytes 24584 | tf_op jit(solution)/shard_map/ppermute | solution.py:45
  155.3 17.9 %collective-permute-start.6 = (f32[1,32,128]{2,1,0:T(8,128)S(1)}, f32[1,32,128]{2,1,0:T(8,128)S(1)}, u32[]{:S(2)}, u32[]{:S(2)}) collective-permute-start(f32[1,32,128]{2,1,0:T(8,128)S(1)} %get-tuple-element.168), channel_id=1, source_target_pairs={{32,0},{64,32},{96,64},{128,96},{160,128},{192,160},{224,192},{256... | collective-permute-start | bytes 49160 | tf_op jit(solution)/shard_map/ppermute | solution.py:46
  156.6 16.6 %collective-permute-start.7 = (f32[1,32,128]{2,1,0:T(8,128)S(1)}, f32[1,32,128]{2,1,0:T(8,128)S(1)}, u32[]{:S(2)}, u32[]{:S(2)}) collective-permute-start(f32[1,32,128]{2,1,0:T(8,128)S(1)} %get-tuple-element.167), channel_id=1, source_target_pairs={{0,32},{32,64},{64,96},{96,128},{128,160},{160,192},{192,224},{224... | collective-permute-start | bytes 49160 | tf_op jit(solution)/shard_map/ppermute | solution.py:45
  160.7 8.6 %collective-permute-start.11 = (f32[16,32,1]{2,1,0:T(8,128)S(1)}, f32[16,32,1]{2,1,0:T(8,128)S(1)}, u32[]{:S(2)}, u32[]{:S(2)}) collective-permute-start(f32[16,32,1]{2,1,0:T(8,128)S(1)} %get-tuple-element.166), channel_id=1, source_target_pairs={{0,1},{1,2},{2,3},{4,5},{5,6},{6,7},{8,9},{9,10},{10,11},{12,13},{... | collective-permute-start | bytes 6152 | tf_op jit(solution)/shard_map/ppermute | solution.py:45
  163.4 9.8 %collective-permute-start.10 = (f32[16,32,1]{2,1,0:T(8,128)S(1)}, f32[16,32,1]{2,1,0:T(8,128)S(1)}, u32[]{:S(2)}, u32[]{:S(2)}) collective-permute-start(f32[16,32,1]{2,1,0:T(8,128)S(1)} %get-tuple-element.165), channel_id=1, source_target_pairs={{1,0},{2,1},{3,2},{5,4},{6,5},{7,6},{9,8},{10,9},{11,10},{13,12},{... | collective-permute-start | bytes 6152 | tf_op jit(solution)/shard_map/ppermute | solution.py:46
  173.7 13.8 %collective-permute-start.14 = (f32[16,1,128]{2,1,0:T(1,128)S(1)}, f32[16,1,128]{2,1,0:T(1,128)S(1)}, u32[]{:S(2)}, u32[]{:S(2)}) collective-permute-start(f32[16,1,128]{2,1,0:T(1,128)S(1)} %get-tuple-element.164), channel_id=1, source_target_pairs={{4,0},{8,4},{12,8},{16,12},{20,16},{24,20},{28,24},{5,1},{9,5},{13... | collective-permute-start | bytes 24584 | tf_op jit(solution)/shard_map/ppermute | solution.py:46
  176.4 12.3 %collective-permute-start.15 = (f32[16,1,128]{2,1,0:T(1,128)S(1)}, f32[16,1,128]{2,1,0:T(1,128)S(1)}, u32[]{:S(2)}, u32[]{:S(2)}) collective-permute-start(f32[16,1,128]{2,1,0:T(1,128)S(1)} %get-tuple-element.163), channel_id=1, source_target_pairs={{0,4},{4,8},{8,12},{12,16},{16,20},{20,24},{24,28},{1,5},{5,9},{9,... | collective-permute-start | bytes 24584 | tf_op jit(solution)/shard_map/ppermute | solution.py:45
  179.4 17.5 %collective-permute-start.12 = (f32[1,32,128]{2,1,0:T(8,128)S(1)}, f32[1,32,128]{2,1,0:T(8,128)S(1)}, u32[]{:S(2)}, u32[]{:S(2)}) collective-permute-start(f32[1,32,128]{2,1,0:T(8,128)S(1)} %get-tuple-element.162), channel_id=1, source_target_pairs={{32,0},{64,32},{96,64},{128,96},{160,128},{192,160},{224,192},{256... | collective-permute-start | bytes 49160 | tf_op jit(solution)/shard_map/ppermute | solution.py:46
  180.7 16.2 %collective-permute-start.13 = (f32[1,32,128]{2,1,0:T(8,128)S(1)}, f32[1,32,128]{2,1,0:T(8,128)S(1)}, u32[]{:S(2)}, u32[]{:S(2)}) collective-permute-start(f32[1,32,128]{2,1,0:T(8,128)S(1)} %get-tuple-element.161), channel_id=1, source_target_pairs={{0,32},{32,64},{64,96},{96,128},{128,160},{160,192},{192,224},{224... | collective-permute-start | bytes 49160 | tf_op jit(solution)/shard_map/ppermute | solution.py:45
  187.4 9.5 %collective-permute-start.16 = (f32[16,32,1]{2,1,0:T(8,128)S(1)}, f32[16,32,1]{2,1,0:T(8,128)S(1)}, u32[]{:S(2)}, u32[]{:S(2)}) collective-permute-start(f32[16,32,1]{2,1,0:T(8,128)S(1)} %get-tuple-element.159), channel_id=1, source_target_pairs={{1,0},{2,1},{3,2},{5,4},{6,5},{7,6},{9,8},{10,9},{11,10},{13,12},{... | collective-permute-start | bytes 6152 | tf_op jit(solution)/shard_map/ppermute | solution.py:46
  197.3 15.2 %collective-permute-start.20 = (f32[16,1,128]{2,1,0:T(1,128)S(1)}, f32[16,1,128]{2,1,0:T(1,128)S(1)}, u32[]{:S(2)}, u32[]{:S(2)}) collective-permute-start(f32[16,1,128]{2,1,0:T(1,128)S(1)} %get-tuple-element.156), channel_id=1, source_target_pairs={{4,0},{8,4},{12,8},{16,12},{20,16},{24,20},{28,24},{5,1},{9,5},{13... | collective-permute-start | bytes 24584 | tf_op jit(solution)/shard_map/ppermute | solution.py:46
  200.4 22.0 %collective-permute-start.18 = (f32[1,32,128]{2,1,0:T(8,128)S(1)}, f32[1,32,128]{2,1,0:T(8,128)S(1)}, u32[]{:S(2)}, u32[]{:S(2)}) collective-permute-start(f32[1,32,128]{2,1,0:T(8,128)S(1)} %get-tuple-element.158), channel_id=1, source_target_pairs={{32,0},{64,32},{96,64},{128,96},{160,128},{192,160},{224,192},{256... | collective-permute-start | bytes 49160 | tf_op jit(solution)/shard_map/ppermute | solution.py:46
  201.7 20.7 %collective-permute-start.19 = (f32[1,32,128]{2,1,0:T(8,128)S(1)}, f32[1,32,128]{2,1,0:T(8,128)S(1)}, u32[]{:S(2)}, u32[]{:S(2)}) collective-permute-start(f32[1,32,128]{2,1,0:T(8,128)S(1)} %get-tuple-element.157), channel_id=1, source_target_pairs={{0,32},{32,64},{64,96},{96,128},{128,160},{160,192},{192,224},{224... | collective-permute-start | bytes 49160 | tf_op jit(solution)/shard_map/ppermute | solution.py:45
  209.3 8.8 %collective-permute-start.23 = (f32[16,32,1]{2,1,0:T(8,128)S(1)}, f32[16,32,1]{2,1,0:T(8,128)S(1)}, u32[]{:S(2)}, u32[]{:S(2)}) collective-permute-start(f32[16,32,1]{2,1,0:T(8,128)S(1)} %get-tuple-element.154), channel_id=1, source_target_pairs={{0,1},{1,2},{2,3},{4,5},{5,6},{6,7},{8,9},{9,10},{10,11},{12,13},{... | collective-permute-start | bytes 6152 | tf_op jit(solution)/shard_map/ppermute | solution.py:45
  212.6 9.8 %collective-permute-start.22 = (f32[16,32,1]{2,1,0:T(8,128)S(1)}, f32[16,32,1]{2,1,0:T(8,128)S(1)}, u32[]{:S(2)}, u32[]{:S(2)}) collective-permute-start(f32[16,32,1]{2,1,0:T(8,128)S(1)} %get-tuple-element.153), channel_id=1, source_target_pairs={{1,0},{2,1},{3,2},{5,4},{6,5},{7,6},{9,8},{10,9},{11,10},{13,12},{... | collective-permute-start | bytes 6152 | tf_op jit(solution)/shard_map/ppermute | solution.py:46
  340.8 20.0 %all-to-all-start.3 = ((f32[32,1,4096]{2,1,0:T(1,128)}), f32[32,1,4096]{2,1,0:T(1,128)S(1)}, u32[]{:S(2)}, u32[]{:S(2)}) async-start(f32[32,1,4096]{2,1,0:T(1,128)} %copy.463), calls=%async_computation.3 | async-start | bytes 1048576 | tf_op jit(solution)/shard_map/all_to_all | solution.py:182
  345.1 14.3 %collective-permute-start.26 = (f32[16,1,128]{2,1,0:T(1,128)S(1)}, f32[16,1,128]{2,1,0:T(1,128)S(1)}, u32[]{:S(2)}, u32[]{:S(2)}) collective-permute-start(f32[16,1,128]{2,1,0:T(1,128)S(1)} %get-tuple-element.152), channel_id=1, source_target_pairs={{4,0},{8,4},{12,8},{16,12},{20,16},{24,20},{28,24},{5,1},{9,5},{13... | collective-permute-start | bytes 24584 | tf_op jit(solution)/shard_map/ppermute | solution.py:46
  347.3 13.5 %collective-permute-start.27 = (f32[16,1,128]{2,1,0:T(1,128)S(1)}, f32[16,1,128]{2,1,0:T(1,128)S(1)}, u32[]{:S(2)}, u32[]{:S(2)}) collective-permute-start(f32[16,1,128]{2,1,0:T(1,128)S(1)} %get-tuple-element.151), channel_id=1, source_target_pairs={{0,4},{4,8},{8,12},{12,16},{16,20},{20,24},{24,28},{1,5},{5,9},{9,... | collective-permute-start | bytes 24584 | tf_op jit(solution)/shard_map/ppermute | solution.py:45
  350.8 31.7 %collective-permute-start.29 = (f32[16,32,1]{2,1,0:T(8,128)S(1)}, f32[16,32,1]{2,1,0:T(8,128)S(1)}, u32[]{:S(2)}, u32[]{:S(2)}) collective-permute-start(f32[16,32,1]{2,1,0:T(8,128)S(1)} %get-tuple-element.148), channel_id=1, source_target_pairs={{0,1},{1,2},{2,3},{4,5},{5,6},{6,7},{8,9},{9,10},{10,11},{12,13},{... | collective-permute-start | bytes 6152 | tf_op jit(solution)/shard_map/ppermute | solution.py:45
  354.1 28.5 %collective-permute-start.24 = (f32[1,32,128]{2,1,0:T(8,128)S(1)}, f32[1,32,128]{2,1,0:T(8,128)S(1)}, u32[]{:S(2)}, u32[]{:S(2)}) collective-permute-start(f32[1,32,128]{2,1,0:T(8,128)S(1)} %get-tuple-element.150), channel_id=1, source_target_pairs={{32,0},{64,32},{96,64},{128,96},{160,128},{192,160},{224,192},{256... | collective-permute-start | bytes 49160 | tf_op jit(solution)/shard_map/ppermute | solution.py:46
  355.4 27.2 %collective-permute-start.25 = (f32[1,32,128]{2,1,0:T(8,128)S(1)}, f32[1,32,128]{2,1,0:T(8,128)S(1)}, u32[]{:S(2)}, u32[]{:S(2)}) collective-permute-start(f32[1,32,128]{2,1,0:T(8,128)S(1)} %get-tuple-element.149), channel_id=1, source_target_pairs={{0,32},{32,64},{64,96},{96,128},{128,160},{160,192},{192,224},{224... | collective-permute-start | bytes 49160 | tf_op jit(solution)/shard_map/ppermute | solution.py:45
  359.4 23.1 %collective-permute-start.28 = (f32[16,32,1]{2,1,0:T(8,128)S(1)}, f32[16,32,1]{2,1,0:T(8,128)S(1)}, u32[]{:S(2)}, u32[]{:S(2)}) collective-permute-start(f32[16,32,1]{2,1,0:T(8,128)S(1)} %get-tuple-element.147), channel_id=1, source_target_pairs={{1,0},{2,1},{3,2},{5,4},{6,5},{7,6},{9,8},{10,9},{11,10},{13,12},{... | collective-permute-start | bytes 6152 | tf_op jit(solution)/shard_map/ppermute | solution.py:46
  383.0 15.0 %collective-permute-start.32 = (f32[16,1,128]{2,1,0:T(1,128)S(1)}, f32[16,1,128]{2,1,0:T(1,128)S(1)}, u32[]{:S(2)}, u32[]{:S(2)}) collective-permute-start(f32[16,1,128]{2,1,0:T(1,128)S(1)} %get-tuple-element.146), channel_id=1, source_target_pairs={{4,0},{8,4},{12,8},{16,12},{20,16},{24,20},{28,24},{5,1},{9,5},{13... | collective-permute-start | bytes 24584 | tf_op jit(solution)/shard_map/ppermute | solution.py:46
  385.0 14.4 %collective-permute-start.33 = (f32[16,1,128]{2,1,0:T(1,128)S(1)}, f32[16,1,128]{2,1,0:T(1,128)S(1)}, u32[]{:S(2)}, u32[]{:S(2)}) collective-permute-start(f32[16,1,128]{2,1,0:T(1,128)S(1)} %get-tuple-element.145), channel_id=1, source_target_pairs={{0,4},{4,8},{8,12},{12,16},{16,20},{20,24},{24,28},{1,5},{5,9},{9,... | collective-permute-start | bytes 24584 | tf_op jit(solution)/shard_map/ppermute | solution.py:45
  388.6 19.3 %collective-permute-start.30 = (f32[1,32,128]{2,1,0:T(8,128)S(1)}, f32[1,32,128]{2,1,0:T(8,128)S(1)}, u32[]{:S(2)}, u32[]{:S(2)}) collective-permute-start(f32[1,32,128]{2,1,0:T(8,128)S(1)} %get-tuple-element.144), channel_id=1, source_target_pairs={{32,0},{64,32},{96,64},{128,96},{160,128},{192,160},{224,192},{256... | collective-permute-start | bytes 49160 | tf_op jit(solution)/shard_map/ppermute | solution.py:46
  389.9 18.0 %collective-permute-start.31 = (f32[1,32,128]{2,1,0:T(8,128)S(1)}, f32[1,32,128]{2,1,0:T(8,128)S(1)}, u32[]{:S(2)}, u32[]{:S(2)}) collective-permute-start(f32[1,32,128]{2,1,0:T(8,128)S(1)} %get-tuple-element.143), channel_id=1, source_target_pairs={{0,32},{32,64},{64,96},{96,128},{128,160},{160,192},{192,224},{224... | collective-permute-start | bytes 49160 | tf_op jit(solution)/shard_map/ppermute | solution.py:45
  394.0 10.0 %collective-permute-start.35 = (f32[16,32,1]{2,1,0:T(8,128)S(1)}, f32[16,32,1]{2,1,0:T(8,128)S(1)}, u32[]{:S(2)}, u32[]{:S(2)}) collective-permute-start(f32[16,32,1]{2,1,0:T(8,128)S(1)} %get-tuple-element.142), channel_id=1, source_target_pairs={{0,1},{1,2},{2,3},{4,5},{5,6},{6,7},{8,9},{9,10},{10,11},{12,13},{... | collective-permute-start | bytes 6152 | tf_op jit(solution)/shard_map/ppermute | solution.py:45
  398.1 9.9 %collective-permute-start.34 = (f32[16,32,1]{2,1,0:T(8,128)S(1)}, f32[16,32,1]{2,1,0:T(8,128)S(1)}, u32[]{:S(2)}, u32[]{:S(2)}) collective-permute-start(f32[16,32,1]{2,1,0:T(8,128)S(1)} %get-tuple-element.141), channel_id=1, source_target_pairs={{1,0},{2,1},{3,2},{5,4},{6,5},{7,6},{9,8},{10,9},{11,10},{13,12},{... | collective-permute-start | bytes 6152 | tf_op jit(solution)/shard_map/ppermute | solution.py:46
  408.4 14.2 %collective-permute-start.38 = (f32[16,1,128]{2,1,0:T(1,128)S(1)}, f32[16,1,128]{2,1,0:T(1,128)S(1)}, u32[]{:S(2)}, u32[]{:S(2)}) collective-permute-start(f32[16,1,128]{2,1,0:T(1,128)S(1)} %get-tuple-element.140), channel_id=1, source_target_pairs={{4,0},{8,4},{12,8},{16,12},{20,16},{24,20},{28,24},{5,1},{9,5},{13... | collective-permute-start | bytes 24584 | tf_op jit(solution)/shard_map/ppermute | solution.py:46
  411.0 12.9 %collective-permute-start.39 = (f32[16,1,128]{2,1,0:T(1,128)S(1)}, f32[16,1,128]{2,1,0:T(1,128)S(1)}, u32[]{:S(2)}, u32[]{:S(2)}) collective-permute-start(f32[16,1,128]{2,1,0:T(1,128)S(1)} %get-tuple-element.139), channel_id=1, source_target_pairs={{0,4},{4,8},{8,12},{12,16},{16,20},{20,24},{24,28},{1,5},{5,9},{9,... | collective-permute-start | bytes 24584 | tf_op jit(solution)/shard_map/ppermute | solution.py:45
  414.0 18.0 %collective-permute-start.36 = (f32[1,32,128]{2,1,0:T(8,128)S(1)}, f32[1,32,128]{2,1,0:T(8,128)S(1)}, u32[]{:S(2)}, u32[]{:S(2)}) collective-permute-start(f32[1,32,128]{2,1,0:T(8,128)S(1)} %get-tuple-element.138), channel_id=1, source_target_pairs={{32,0},{64,32},{96,64},{128,96},{160,128},{192,160},{224,192},{256... | collective-permute-start | bytes 49160 | tf_op jit(solution)/shard_map/ppermute | solution.py:46
  415.3 16.7 %collective-permute-start.37 = (f32[1,32,128]{2,1,0:T(8,128)S(1)}, f32[1,32,128]{2,1,0:T(8,128)S(1)}, u32[]{:S(2)}, u32[]{:S(2)}) collective-permute-start(f32[1,32,128]{2,1,0:T(8,128)S(1)} %get-tuple-element.137), channel_id=1, source_target_pairs={{0,32},{32,64},{64,96},{96,128},{128,160},{160,192},{192,224},{224... | collective-permute-start | bytes 49160 | tf_op jit(solution)/shard_map/ppermute | solution.py:45
  419.4 8.7 %collective-permute-start.41 = (f32[16,32,1]{2,1,0:T(8,128)S(1)}, f32[16,32,1]{2,1,0:T(8,128)S(1)}, u32[]{:S(2)}, u32[]{:S(2)}) collective-permute-start(f32[16,32,1]{2,1,0:T(8,128)S(1)} %get-tuple-element.136), channel_id=1, source_target_pairs={{0,1},{1,2},{2,3},{4,5},{5,6},{6,7},{8,9},{9,10},{10,11},{12,13},{... | collective-permute-start | bytes 6152 | tf_op jit(solution)/shard_map/ppermute | solution.py:45
  422.5 9.5 %collective-permute-start.40 = (f32[16,32,1]{2,1,0:T(8,128)S(1)}, f32[16,32,1]{2,1,0:T(8,128)S(1)}, u32[]{:S(2)}, u32[]{:S(2)}) collective-permute-start(f32[16,32,1]{2,1,0:T(8,128)S(1)} %get-tuple-element.135), channel_id=1, source_target_pairs={{1,0},{2,1},{3,2},{5,4},{6,5},{7,6},{9,8},{10,9},{11,10},{13,12},{... | collective-permute-start | bytes 6152 | tf_op jit(solution)/shard_map/ppermute | solution.py:46
  432.5 14.9 %collective-permute-start.44 = (f32[16,1,128]{2,1,0:T(1,128)S(1)}, f32[16,1,128]{2,1,0:T(1,128)S(1)}, u32[]{:S(2)}, u32[]{:S(2)}) collective-permute-start(f32[16,1,128]{2,1,0:T(1,128)S(1)} %get-tuple-element.132), channel_id=1, source_target_pairs={{4,0},{8,4},{12,8},{16,12},{20,16},{24,20},{28,24},{5,1},{9,5},{13... | collective-permute-start | bytes 24584 | tf_op jit(solution)/shard_map/ppermute | solution.py:46
  435.5 21.8 %collective-permute-start.42 = (f32[1,32,128]{2,1,0:T(8,128)S(1)}, f32[1,32,128]{2,1,0:T(8,128)S(1)}, u32[]{:S(2)}, u32[]{:S(2)}) collective-permute-start(f32[1,32,128]{2,1,0:T(8,128)S(1)} %get-tuple-element.134), channel_id=1, source_target_pairs={{32,0},{64,32},{96,64},{128,96},{160,128},{192,160},{224,192},{256... | collective-permute-start | bytes 49160 | tf_op jit(solution)/shard_map/ppermute | solution.py:46
  436.8 20.5 %collective-permute-start.43 = (f32[1,32,128]{2,1,0:T(8,128)S(1)}, f32[1,32,128]{2,1,0:T(8,128)S(1)}, u32[]{:S(2)}, u32[]{:S(2)}) collective-permute-start(f32[1,32,128]{2,1,0:T(8,128)S(1)} %get-tuple-element.133), channel_id=1, source_target_pairs={{0,32},{32,64},{64,96},{96,128},{128,160},{160,192},{192,224},{224... | collective-permute-start | bytes 49160 | tf_op jit(solution)/shard_map/ppermute | solution.py:45
  444.5 8.5 %collective-permute-start.47 = (f32[16,32,1]{2,1,0:T(8,128)S(1)}, f32[16,32,1]{2,1,0:T(8,128)S(1)}, u32[]{:S(2)}, u32[]{:S(2)}) collective-permute-start(f32[16,32,1]{2,1,0:T(8,128)S(1)} %get-tuple-element.130), channel_id=1, source_target_pairs={{0,1},{1,2},{2,3},{4,5},{5,6},{6,7},{8,9},{9,10},{10,11},{12,13},{... | collective-permute-start | bytes 6152 | tf_op jit(solution)/shard_map/ppermute | solution.py:45
  447.4 9.9 %collective-permute-start.46 = (f32[16,32,1]{2,1,0:T(8,128)S(1)}, f32[16,32,1]{2,1,0:T(8,128)S(1)}, u32[]{:S(2)}, u32[]{:S(2)}) collective-permute-start(f32[16,32,1]{2,1,0:T(8,128)S(1)} %get-tuple-element.129), channel_id=1, source_target_pairs={{1,0},{2,1},{3,2},{5,4},{6,5},{7,6},{9,8},{10,9},{11,10},{13,12},{... | collective-permute-start | bytes 6152 | tf_op jit(solution)/shard_map/ppermute | solution.py:46
  465.8 102.2 %all-to-all-start.4 = ((f32[32,1,4097]{2,1,0:T(1,128)}), f32[32,1,4097]{2,1,0:T(1,128)S(1)}, u32[]{:S(2)}, u32[]{:S(2)}) async-start(f32[32,1,4097]{2,1,0:T(1,128)} %copy.468), calls=%async_computation.4 | async-start | bytes 1081344 | tf_op jit(solution)/shard_map/all_to_all | solution.py:30
  (17 other events, 139.4 us)
where the time goes:
time: 601 us; the launch traced here: 589 us
  local copies, waits for them, and re-layouts  157 us (26%)
  starting transfers between devices  153 us (25%)
  blocking collectives  109 us (18%)
  other arithmetic  64.8 us (11%)
  waiting for transfers between devices  60.4 us (10%)
  matrix products  39.9 us (7%)
    psum x4, blocking collectives, by_axis(): return functools.reduce(lax.psum, axes, array)  93.1 us
    ppermute x24, starting transfers between devices, with_halo(): lax.ppermute(last, axis, up)  80.1 us
    ppermute x24, starting transfers between devices, with_halo(): lax.ppermute(initial, axis, [(b, a) for a, b in up])  54.8 us
    broadcast_in_dim x8, local copies, waits for them, and re-layouts, inject(): spread = jnp.broadcast_to(shaped, (number, FOOT, 2, FOOT, 2, FOOT, 2))  45 us
    reshape x4, local copies, waits for them, and re-layouts, inject(): return spread.reshape(number, 8 * FOOT * FOOT * FOOT)  38 us
    dot_general x2, matrix products, local(): jnp.dot(deposit, returned, precision=HIGHEST)  32.7 us
    reduce_sum x2, other arithmetic, restrict(): return values.reshape(number, FOOT, 2, FOOT, 2, FOOT, 2).mean(axis=(2, 4,...  27.7 us
    ppermute x24, waiting for transfers between devices, with_halo(): lax.ppermute(last, axis, up)  26.1 us
  transfers between devices with their start and end apart: 52, of which 15 were waited for; matrix products, arithmetic and copies ran while one was open for 21% of the time, Pallas kernels for 0%

commit v1 on v0

v1 whole, which is shorter than its diff:
```python
import functools

import jax
import jax.numpy as jnp
from jax import lax
from jax.experimental import pallas as pl
from jax.experimental.pallas import tpu as pltpu
from jax.sharding import PartitionSpec as P

FOOT = 16
CYCLES = 2
CSWEEPS = 4
FSWEEPS = 3
SLOTS = 4
OMEGA = 0.8
HIGHEST = lax.Precision.HIGHEST
F32 = jnp.float32
MESH = pl.DeviceIdType.MESH

ROWS = 512
FROWS = 1024
SWEEPS = CYCLES * CSWEEPS


def lane_roll(array, shift):
    return pltpu.roll(array, shift % 128, 1)


def group_transpose(parts):
    group = lax.broadcasted_iota(jnp.int32, (8, 128), 1) // 16
    parts = list(parts)
    for step in (1, 2, 4):
        clear = (group & step) == 0
        for i in range(8):
            if i & step:
                continue
            a, b = parts[i], parts[i + step]
            parts[i] = jnp.where(clear, a, lane_roll(b, 16 * step))
            parts[i + step] = jnp.where(clear, lane_roll(a, -16 * step), b)
    return parts


def kernel(
    sizes,
    corner,
    owner,
    source_hbm,
    shift_hbm,
    start_hbm,
    fsource_hbm,
    fshift_hbm,
    fstart_hbm,
    pot_out,
    fine_out,
    norm_out,
    pot,
    source,
    diag,
    weight,
    comp,
    xlo,
    xhi,
    ylo,
    yhi,
    zlo,
    zhi,
    yface,
    zface,
    fine,
    fsource,
    fdiag,
    fweight,
    expand,
    gather,
    dense,
    ghost,
    wide,
    packed,
    mixed,
    rblocks,
    code,
    count,
    place_of,
    flag_out,
    flag_in,
    d_out,
    d_in,
    r_out,
    r_in,
    csum,
    fsum,
    nx_in,
    np_in,
    n_send,
    local_sem,
    flag_sem,
    d_send,
    d_recv,
    r_send,
    r_recv,
    h_send,
    h_recv,
    n_sem,
    chain,
):
    n_x, n_y, n_z, cells = sizes
    members = n_y * n_z
    gx, gy, gz = lax.axis_index("gx"), lax.axis_index("gy"), lax.axis_index("gz")
    me = gy * n_z + gz

    def peer(q):
        return {"gy": q // n_z, "gz": lax.rem(q, n_z)}

    loads = [
        pltpu.make_async_copy(start_hbm, pot.at[0], local_sem.at[0]),
        pltpu.make_async_copy(source_hbm, source, local_sem.at[1]),
        pltpu.make_async_copy(shift_hbm, diag, local_sem.at[2]),
        pltpu.make_async_copy(fsource_hbm, fsource, local_sem.at[3]),
        pltpu.make_async_copy(fshift_hbm, fdiag, local_sem.at[4]),
        pltpu.make_async_copy(fstart_hbm, fine.at[0], local_sem.at[5]),
    ]
    for load in loads:
        load.start()

    barrier = pltpu.get_barrier_semaphore()

    def greet(i, carry):
        q = lax.rem(me + i, members)
        pl.semaphore_signal(barrier, inc=1, device_id=peer(q), device_id_type=MESH)
        return carry

    lax.fori_loop(1, members, greet, 0)

    def ring(distance):
        return lax.rem(gx + distance + n_x, n_x)

    for way in (1, -1):
        pl.semaphore_signal(barrier, inc=1, device_id={"gx": ring(way)}, device_id_type=MESH)

    owners = [owner[0, s] for s in range(SLOTS)]
    lives = [(o >= 0) & (o < members) for o in owners]
    places = [
        jnp.where(
            lives[s],
            ((corner[0, s, 1] >> 5) & 1) * 8 + ((corner[0, s, 2] >> 5) & 7),
            -1,
        )
        for s in range(SLOTS)
    ]
    for q in range(members):
        spot = jnp.int32(0)
        flag = jnp.int32(0)
        for s in range(SLOTS):
            mine = owners[s] == q
            spot = jnp.where(mine, places[s], spot)
            flag = jnp.where(mine, 1, flag)
        place_of[q] = spot
        flag_out[q] = jnp.full((1, 128), flag.astype(F32), F32)

    lane8 = lax.broadcasted_iota(jnp.int32, (8, 128), 1)
    sub8 = lax.broadcasted_iota(jnp.int32, (8, 128), 0)
    lane32 = lax.broadcasted_iota(jnp.int32, (32, 128), 1)
    row32 = lax.broadcasted_iota(jnp.int32, (32, 128), 0)
    low4 = sub8 < 4

    zeros = jnp.zeros((32, 128), F32)

    @pl.when(gx == 0)
    def _():
        for k in range(SWEEPS):
            xlo[k] = zeros

    @pl.when(gx == n_x - 1)
    def _():
        for k in range(SWEEPS):
            xhi[k] = zeros

    @pl.when(gy == 0)
    def _():
        for k in range(SWEEPS):
            ylo[k] = zeros[:16]

    @pl.when(gy == n_y - 1)
    def _():
        for k in range(SWEEPS):
            yhi[k] = zeros[:16]

    @pl.when(gz == 0)
    def _():
        for k in range(SWEEPS):
            zlo[k] = zeros[:8]

    @pl.when(gz == n_z - 1)
    def _():
        for k in range(SWEEPS):
            zhi[k] = zeros[:8]

    def halo_copies(k):
        return (
            (gx > 0, pot.at[k, pl.ds(0, 32)], xhi.at[k], 0, {"gx": ring(-1)}),
            (gx < n_x - 1, pot.at[k, pl.ds(ROWS - 32, 32)], xlo.at[k], 1, {"gx": ring(1)}),
            (gy > 0, yface.at[k, 0], yhi.at[k], 2, {"gy": lax.rem(gy + n_y - 1, n_y)}),
            (gy < n_y - 1, yface.at[k, 1], ylo.at[k], 3, {"gy": lax.rem(gy + 1, n_y)}),
            (gz > 0, zface.at[k], zhi.at[k], 4, {"gz": lax.rem(gz + n_z - 1, n_z)}),
            (gz < n_z - 1, zface.at[k], zlo.at[k], 5, {"gz": lax.rem(gz + 1, n_z)}),
        )

    def halo(k, act):
        for i, (there, src, dst, sem, device) in enumerate(halo_copies(k)):
            copy = pltpu.make_async_remote_copy(
                src_ref=src,
                dst_ref=dst,
                send_sem=h_send.at[k, sem],
                recv_sem=h_recv.at[k, sem],
                device_id=device,
                device_id_type=MESH,
            )
            if act == "recv":
                there = halo_copies(k)[i ^ 1][0]

            @pl.when(there)
            def _(copy=copy):
                if act == "start":
                    copy.start()
                elif act == "recv":
                    copy.wait_recv()
                else:
                    copy.wait_send()

    def faces_of(x, slab, k, acc):
        yface[k, 0, pl.ds(x, 1), :] = slab[0:1]
        yface[k, 1, pl.ds(x, 1), :] = slab[31:32]
        for t in range(4):
            v = x * 4 + t
            keep = (lane8 == 2 * v) | (lane8 == (2 * v - 1) % 128)
            acc = jnp.where(keep, lane_roll(slab[8 * t : 8 * t + 8], 2 * v), acc)
        return acc

    def send_parents(c):
        for x in range(16):
            slab = pot[c * CSWEEPS, pl.ds(x * 32, 32), :]
            before = pot[jnp.maximum(c - 1, 0) * CSWEEPS, pl.ds(x * 32, 32), :]
            slab = jnp.where(c > 0, slab - before, slab)
            for by in range(2):
                for y3 in range(2):
                    t = by * 2 + y3
                    mixed[pl.ds(by * 32 + x * 2 + y3, 8, stride=64), :] = slab[8 * t : 8 * t + 8]
        for by in range(2):
            for i in range(4):
                parts = [mixed[pl.ds(k * 64 + by * 32 + 8 * i, 8), :] for k in range(8)]
                for bz, part in enumerate(group_transpose(parts)):
                    packed[by * 8 + bz, pl.ds(8 * i, 8), :] = part

        d_in[c, me] = packed[place_of[me]]

        def send(i, carry):
            q = lax.rem(me + i, members)
            d_out[c, q] = packed[place_of[q]]
            pltpu.make_async_remote_copy(
                src_ref=d_out.at[c, q],
                dst_ref=d_in.at[c, me],
                send_sem=d_send.at[c],
                recv_sem=d_recv.at[c],
                device_id=peer(q),
                device_id_type=MESH,
            ).start()
            return carry

        lax.fori_loop(1, members, send, 0)

    def wait_all(buffer, sem):
        part = buffer.at[pl.ds(0, members - 1)]
        pltpu.make_async_copy(part, part, sem).wait()

    def recv_parents(c):
        wait_all(d_in.at[c], d_recv.at[c])

        def pick(r, acc):
            mark = code[r]
            acc = list(acc)
            for i in range(4):
                data = d_in[c, r, pl.ds(8 * i, 8), :]
                for j in range(SLOTS):
                    acc[j * 4 + i] = jnp.where(mark == j, data, acc[j * 4 + i])
            return tuple(acc)

        blank = jnp.zeros((8, 128), F32)
        acc = lax.fori_loop(0, members, pick, (blank,) * 16)
        for j in range(SLOTS):
            for i in range(4):
                dense[pl.ds(32 * i + j, 8, stride=4), :] = acc[j * 4 + i]
        for y2 in range(2):
            a = jnp.dot(
                dense[...], expand[:, pl.ds(256 * y2, 128)], precision=HIGHEST,
                preferred_element_type=F32,
            )
            b = jnp.dot(
                dense[...], expand[:, pl.ds(256 * y2 + 128, 128)], precision=HIGHEST,
                preferred_element_type=F32,
            )
            for x in range(16):
                ax, bx = a[8 * x : 8 * x + 8], b[8 * x : 8 * x + 8]
                ghost[pl.ds(x * 32 + y2 * 8, 8), :] = jnp.where(low4, ax, pltpu.roll(bx, 4, 0))
                ghost[pl.ds(x * 32 + 16 + y2 * 8, 8), :] = jnp.where(low4, pltpu.roll(ax, 4, 0), bx)

    fine_y = (row32 // 4) * 4 + lane32 // 32
    fine_z = lane32 % 32
    sides = (
        (fine_y == 0).astype(F32)
        + (fine_y == 31).astype(F32)
        + (fine_z == 0).astype(F32)
        + (fine_z == 31).astype(F32)
    )

    def use_parents(c):
        for X in range(32):
            g = ghost[pl.ds(X // 2 * 32, 32), :]
            times = sides + 1.0 if X in (0, 31) else sides
            fsource[pl.ds(X * 32, 32), :] = fsource[pl.ds(X * 32, 32), :] + times * g

        @pl.when(c > 0)
        def _():
            for X in range(32):
                at = lax.rem(c, 2)
                fine[at, pl.ds(X * 32, 32), :] = (
                    fine[at, pl.ds(X * 32, 32), :] + ghost[pl.ds(X // 2 * 32, 32), :]
                )

    not_first = fine_z > 0
    not_last = fine_z < 31
    first_group = lane32 < 32
    last_group = lane32 >= 96

    def beside(at, X):
        u = fine[at, pl.ds(X * 32, 32), :]
        after = jnp.where(row32 < 28, pltpu.roll(u, 28, 0), 0.0)
        prior = jnp.where(row32 >= 4, pltpu.roll(u, 4, 0), 0.0)
        total = lane_roll(jnp.where(first_group, after, u), -32)
        total = total + lane_roll(jnp.where(last_group, prior, u), 32)
        total = total + lane_roll(jnp.where(not_first, u, 0.0), -1)
        total = total + lane_roll(jnp.where(not_last, u, 0.0), 1)
        if X > 0:
            total = total + fine[at, pl.ds(X * 32 - 32, 32), :]
        if X < 31:
            total = total + fine[at, pl.ds(X * 32 + 32, 32), :]
        return u, total

    def fine_sweeps(c):
        def sweep(s, carry):
            at = lax.rem(c + s, 2)
            for X in range(32):
                u, total = beside(at, X)
                rows = pl.ds(X * 32, 32)
                fine[1 - at, rows, :] = (1.0 - OMEGA) * u + fweight[rows, :] * (fsource[rows, :] + total)
            return carry

        lax.fori_loop(0, FSWEEPS, sweep, 0)

        at = lax.rem(c + FSWEEPS, 2)
        squares = jnp.zeros((8, 128), F32)
        for x in range(16):
            both = None
            for X in (2 * x, 2 * x + 1):
                u, total = beside(at, X)
                rows = pl.ds(X * 32, 32)
                rem = fsource[rows, :] - fdiag[rows, :] * u + total
                sq = rem * rem
                squares = squares + ((sq[0:8] + sq[8:16]) + (sq[16:24] + sq[24:32]))
                both = rem if both is None else both + rem
            for y2 in range(2):
                lo = both[8 * y2 : 8 * y2 + 8]
                hi = both[16 + 8 * y2 : 24 + 8 * y2]
                wide[pl.ds(8 * x, 8), pl.ds(256 * y2, 128)] = jnp.where(low4, lo, pltpu.roll(hi, 4, 0))
                wide[pl.ds(8 * x, 8), pl.ds(256 * y2 + 128, 128)] = jnp.where(
                    low4, pltpu.roll(lo, 4, 0), hi
                )
        live = (sub8 % 4).astype(F32) < count[...]
        fsum[c] = jnp.where(live, squares, 0.0)
        dense[...] = jnp.dot(
            wide[...], gather[...], precision=HIGHEST, preferred_element_type=F32
        )
        for j in range(SLOTS):
            for i in range(4):
                rblocks[j, pl.ds(8 * i, 8), :] = dense[pl.ds(32 * i + j, 8, stride=4), :]

    def send_restricted(c):
        def block_for(r, i):
            mark = code[r]
            value = rblocks[0, pl.ds(8 * i, 8), :]
            for j in range(1, SLOTS):
                value = jnp.where(mark == j, rblocks[j, pl.ds(8 * i, 8), :], value)
            return value

        for i in range(4):
            r_in[c, me, pl.ds(8 * i, 8), :] = block_for(me, i)

        def send(i, carry):
            q = lax.rem(me + i, members)
            for part in range(4):
                r_out[c, q, pl.ds(8 * part, 8), :] = block_for(q, part)
            pltpu.make_async_remote_copy(
                src_ref=r_out.at[c, q],
                dst_ref=r_in.at[c, me],
                send_sem=r_send.at[c],
                recv_sem=r_recv.at[c],
                device_id=peer(q),
                device_id_type=MESH,
            ).start()
            return carry

        lax.fori_loop(1, members, send, 0)

    def recv_restricted(c):
        wait_all(r_in.at[c], r_recv.at[c])
        blocks = [r_in[c, jnp.clip(o, 0, members - 1)] for o in owners]
        for p in range(16):
            value = zeros
            for s in range(SLOTS):
                value = jnp.where(places[s] == p, blocks[s], value)
            packed[p] = value
        for by in range(2):
            for i in range(4):
                parts = [packed[by * 8 + bz, pl.ds(8 * i, 8), :] for bz in range(8)]
                for k, part in enumerate(group_transpose(parts)):
                    mixed[pl.ds(k * 64 + by * 32 + 8 * i, 8), :] = part
        for x in range(16):
            for t in range(4):
                rows = pl.ds(x * 32 + 8 * t, 8)
                comp[rows, :] = (
                    source[rows, :]
                    + mixed[pl.ds(t // 2 * 32 + x * 2 + t % 2, 8, stride=64), :]
                )

    first_lane = lane32 == 0
    last_lane = lane32 == 127

    def coarse_sweep(c, s):
        k = c * CSWEEPS + s
        halo(k, "recv")
        beyond = jnp.where(lane8 % 2 == 0, zhi[k], zlo[k])
        acc = jnp.zeros((8, 128), F32)
        squares = jnp.zeros((8, 128), F32)
        follow = jnp.minimum(k + 1, SWEEPS)
        for x in range(16):
            rows = pl.ds(x * 32, 32)
            p = pot[k, rows, :]
            total = pot[k, pl.ds(x * 32 - 32, 32), :] if x > 0 else xlo[k]
            total = total + (pot[k, pl.ds(x * 32 + 32, 32), :] if x < 15 else xhi[k])
            above = jnp.broadcast_to(yhi[k, pl.ds(x, 1), :], (32, 128))
            below = jnp.broadcast_to(ylo[k, pl.ds(x, 1), :], (32, 128))
            total = total + jnp.where(row32 == 31, above, pltpu.roll(p, 31, 0))
            total = total + jnp.where(row32 == 0, below, pltpu.roll(p, 1, 0))
            edge = jnp.concatenate(
                [lane_roll(beyond, -2 * (x * 4 + t)) for t in range(4)], axis=0
            )
            total = total + lane_roll(jnp.where(first_lane, edge, p), -1)
            total = total + lane_roll(jnp.where(last_lane, edge, p), 1)
            res = comp[rows, :] - diag[rows, :] * p + total
            sq = res * res
            squares = squares + ((sq[0:8] + sq[8:16]) + (sq[16:24] + sq[24:32]))
            new = p + weight[rows, :] * res
            pot[k + 1, rows, :] = new
            acc = faces_of(x, new, k + 1, acc)
        zface[k + 1] = acc
        csum[c] = squares

        @pl.when(k + 1 < SWEEPS)
        def _():
            halo(k + 1, "start")

    loads[0].wait()
    acc = jnp.zeros((8, 128), F32)
    for x in range(16):
        acc = faces_of(x, pot[0, pl.ds(x * 32, 32), :], 0, acc)
    zface[0] = acc
    pl.semaphore_wait(barrier, members + 1)

    flag_in[me] = flag_out[me]

    def send_flag(i, carry):
        q = lax.rem(me + i, members)
        pltpu.make_async_remote_copy(
            src_ref=flag_out.at[q],
            dst_ref=flag_in.at[me],
            send_sem=flag_sem.at[0],
            recv_sem=flag_sem.at[1],
            device_id=peer(q),
            device_id_type=MESH,
        ).start()
        return carry

    lax.fori_loop(1, members, send_flag, 0)
    halo(0, "start")

    rounds = []
    while 2 ** len(rounds) * 2 <= n_x // 2:
        rounds.append(2 ** len(rounds))

    def chain_step(at):
        if 0 < at <= len(rounds):
            pl.semaphore_wait(chain.at[at - 1], 2)
        if at < len(rounds):
            for way in (1, -1):
                pl.semaphore_signal(
                    chain.at[at],
                    inc=1,
                    device_id={"gx": ring(way * rounds[at])},
                    device_id_type=MESH,
                )

    chain_step(0)

    def prepare():
        i = lax.broadcasted_iota(jnp.int32, (128, 512), 0)
        n = lax.broadcasted_iota(jnp.int32, (128, 512), 1)
        lane = n % 128
        expand[...] = (i == (n // 128) * 32 + (lane // 64) * 16 + (lane % 32) // 2).astype(F32)
        n = lax.broadcasted_iota(jnp.int32, (512, 128), 0)
        o = lax.broadcasted_iota(jnp.int32, (512, 128), 1)
        lane = n % 128
        gather[...] = jnp.where(
            o == (n // 128) * 32 + (lane // 64) * 16 + (lane % 32) // 2, 0.125, 0.0
        )
        loads[2].wait()
        for x in range(16):
            rows = pl.ds(x * 32, 32)
            d = 6.0 + diag[rows, :]
            diag[rows, :] = d
            weight[rows, :] = OMEGA / d
        loads[4].wait()
        for X in range(32):
            rows = pl.ds(X * 32, 32)
            d = 6.0 + fdiag[rows, :]
            fdiag[rows, :] = d
            fweight[rows, :] = OMEGA / d
        for at in (1, 3, 5):
            loads[at].wait()
        wait_all(flag_in, flag_sem.at[1])
        before = jnp.zeros((8, 128), F32)
        for r in range(members):
            flag = jnp.broadcast_to(flag_in[r], (8, 128))
            code[r] = jnp.where(flag > 0.5, before, -1.0)
            before = before + flag
        count[...] = before

    norm_row = lax.broadcasted_iota(jnp.int32, (1, 128), 1)

    def norm_copy(src, dst, sem, device):
        return pltpu.make_async_remote_copy(
            src_ref=src,
            dst_ref=dst,
            send_sem=n_sem.at[sem],
            recv_sem=n_sem.at[sem + 1],
            device_id=device,
            device_id_type=MESH,
        )

    def send_norms():
        parts = [jnp.sum(csum[k] + fsum[k]) for k in range(CYCLES)]
        row = jnp.where(norm_row < 64, parts[0], parts[1])
        n_send[0] = row
        nx_in[gx] = row

        def send(i, carry):
            norm_copy(n_send.at[0], nx_in.at[gx], 0, {"gx": lax.rem(gx + i, n_x)}).start()
            return carry

        lax.fori_loop(1, n_x, send, 0)

    def turn_norms():
        part = nx_in.at[pl.ds(0, n_x - 1)]
        pltpu.make_async_copy(part, part, n_sem.at[1]).wait()
        row = nx_in[0]
        for r in range(1, n_x):
            row = row + nx_in[r]
        n_send[1] = row
        np_in[me] = row

        def send(i, carry):
            norm_copy(n_send.at[1], np_in.at[me], 2, peer(lax.rem(me + i, members))).start()
            return carry

        lax.fori_loop(1, members, send, 0)

    def end_norms():
        wait_all(np_in, n_sem.at[3])
        row = np_in[0]
        for r in range(1, members):
            row = row + np_in[r]
        norm_out[...] = jnp.sqrt(row / cells)

    def cycle(c, carry):
        @pl.when(c == CYCLES)
        def _():
            send_norms()

        send_parents(c)

        @pl.when(c == 0)
        def _():
            prepare()

        recv_parents(c)

        @pl.when(c < CYCLES)
        def _():
            use_parents(c)
            for k in range(CYCLES):

                @pl.when(c == k)
                def _(k=k):
                    chain_step(2 * k + 1)

            fine_sweeps(c)
            send_restricted(c)
            for k in range(CYCLES):

                @pl.when(c == k)
                def _(k=k):
                    chain_step(2 * k + 2)

            recv_restricted(c)

            def sweep(s, carry):
                coarse_sweep(c, s)
                return carry

            lax.fori_loop(0, CSWEEPS, sweep, 0)

        return carry

    lax.fori_loop(0, CYCLES + 1, cycle, 0)

    out_pot = pltpu.make_async_copy(pot.at[SWEEPS], pot_out, local_sem.at[0])
    out_pot.start()
    live = ((row32 % 4).astype(F32) < jnp.concatenate([count[...]] * 4, axis=0)).astype(F32)
    end = CYCLES % 2
    for X in range(32):
        rows = pl.ds(X * 32, 32)
        fine[1 - end, rows, :] = (fine[end, rows, :] + ghost[pl.ds(X // 2 * 32, 32), :]) * live
    out_fine = pltpu.make_async_copy(fine.at[1 - end], fine_out, local_sem.at[1])
    out_fine.start()
    turn_norms()

    wait_all(flag_out, flag_sem.at[0])
    for c in range(CYCLES + 1):
        wait_all(d_out.at[c], d_send.at[c])
    for c in range(CYCLES):
        wait_all(r_out.at[c], r_send.at[c])

    def left(k, carry):
        halo(k, "send")
        return carry

    lax.fori_loop(0, SWEEPS, left, 0)
    part = nx_in.at[pl.ds(0, n_x - 1)]
    pltpu.make_async_copy(part, part, n_sem.at[0]).wait()
    end_norms()
    wait_all(np_in, n_sem.at[2])
    out_pot.wait()
    out_fine.wait()


def local(
    coarse_source,
    coarse_shift,
    coarse_start,
    fine_source,
    fine_shift,
    fine_start,
    box_corner,
    box_owner,
):
    n_x, n_y, n_z = (lax.axis_size(a) for a in ("gx", "gy", "gz"))
    members = n_y * n_z
    cells = float(n_x * n_y * n_z * coarse_source.size)

    def fine_rows(array):
        return array.reshape(SLOTS, 256, 128).transpose(1, 0, 2).reshape(FROWS, 128)

    hbm = pl.BlockSpec(memory_space=pltpu.HBM)
    smem = pl.BlockSpec(memory_space=pltpu.SMEM)
    vmem = pl.BlockSpec(memory_space=pltpu.VMEM)

    def buf(*shape):
        return pltpu.VMEM(shape, F32)

    sems = pltpu.SemaphoreType.DMA
    pot, fine, norms = pl.pallas_call(
        functools.partial(kernel, (n_x, n_y, n_z, cells)),
        out_shape=(
            jax.ShapeDtypeStruct((ROWS, 128), F32),
            jax.ShapeDtypeStruct((FROWS, 128), F32),
            jax.ShapeDtypeStruct((1, 128), F32),
        ),
        in_specs=[smem, smem] + [hbm] * 6,
        out_specs=(hbm, hbm, vmem),
        scratch_shapes=[
            buf(SWEEPS + 1, ROWS, 128),
            buf(ROWS, 128),
            buf(ROWS, 128),
            buf(ROWS, 128),
            buf(ROWS, 128),
            buf(SWEEPS, 32, 128),
            buf(SWEEPS, 32, 128),
            buf(SWEEPS, 16, 128),
            buf(SWEEPS, 16, 128),
            buf(SWEEPS, 8, 128),
            buf(SWEEPS, 8, 128),
            buf(SWEEPS + 1, 2, 16, 128),
            buf(SWEEPS + 1, 8, 128),
            buf(2, FROWS, 128),
            buf(FROWS, 128),
            buf(FROWS, 128),
            buf(FROWS, 128),
            buf(128, 512),
            buf(512, 128),
            buf(128, 128),
            buf(ROWS, 128),
            buf(128, 512),
            buf(16, 32, 128),
            buf(ROWS, 128),
            buf(SLOTS, 32, 128),
            buf(members, 8, 128),
            buf(8, 128),
            pltpu.SMEM((members,), jnp.int32),
            buf(members, 1, 128),
            buf(members, 1, 128),
            buf(CYCLES + 1, members, 32, 128),
            buf(CYCLES + 1, members, 32, 128),
            buf(CYCLES, members, 32, 128),
            buf(CYCLES, members, 32, 128),
            buf(CYCLES, 8, 128),
            buf(CYCLES, 8, 128),
            buf(n_x, 1, 128),
            buf(members, 1, 128),
            buf(2, 1, 128),
            sems((6,)),
            sems((2,)),
            sems((CYCLES + 1,)),
            sems((CYCLES + 1,)),
            sems((CYCLES,)),
            sems((CYCLES,)),
            sems((SWEEPS, 6)),
            sems((SWEEPS, 6)),
            sems((4,)),
            pltpu.SemaphoreType.REGULAR((4,)),
        ],
        compiler_params=pltpu.CompilerParams(
            collective_id=0, has_side_effects=True, vmem_limit_bytes=60 * 1000 * 1000
        ),
        name="cycles",
    )(
        box_corner,
        box_owner,
        coarse_source.reshape(ROWS, 128),
        coarse_shift.reshape(ROWS, 128),
        coarse_start.reshape(ROWS, 128),
        fine_rows(fine_source),
        fine_rows(fine_shift),
        fine_rows(fine_start),
    )
    fine = fine.reshape(256, SLOTS, 128).transpose(1, 0, 2).reshape(SLOTS, 256 * 128)
    return pot.reshape(coarse_source.shape), fine, norms[0, ::64]


def solution(mesh):
    every = ("gx", "gy", "gz")
    return jax.shard_map(
        local,
        mesh=mesh,
        in_specs=(
            P("gx", "gy", "gz"),
            P("gx", "gy", "gz"),
            P("gx", "gy", "gz"),
            P(every, None),
            P(every, None),
            P(every, None),
            P(every, None, None),
            P(every, None),
        ),
        out_specs=(P("gx", "gy", "gz"), P(every, None), P()),
        check_vma=False,
    )
```

time: 601 us -> 118 us (0.20); the launches traced: 589 us -> 118 us
  starting transfers between devices: 153 us -> 0 us
  local copies, waits for them, and re-layouts: 157 us -> 5.12 us
  Pallas kernels: 0 us -> 112 us
  blocking collectives: 109 us -> 0 us
  other arithmetic: 64.8 us -> 0 us
  waiting for transfers between devices: 60.4 us -> 0 us
  matrix products: 39.9 us -> 0 us
    ppermute x48 -> x0, starting transfers between devices: 135 us -> none  [the longest x24 80.1 us: with_halo(): lax.ppermute(last, axis, up)]
    pallas_call x0 -> x1, Pallas kernels: none -> 112 us  [local(): pl.pallas_call(functools.partial(kernel, (n_x, n_y, n_z, cells)), out_sha...]
    psum x4 -> x0, blocking collectives: 93.1 us -> none  [by_axis(): return functools.reduce(lax.psum, axes, array)]
    reshape x15 -> x0, local copies, waits for them, and re-layouts: 62.8 us -> none  [the longest x4 38 us: inject(): return spread.reshape(number, 8 * FOOT * FOOT * FOOT)]
    ppermute x48 -> x0, waiting for transfers between devices: 50.7 us -> none  [the longest x24 26.1 us: with_halo(): lax.ppermute(last, axis, up)]
    broadcast_in_dim x9 -> x0, local copies, waits for them, and re-layouts: 45.1 us -> none  [the longest x8 45 us: inject(): spread = jnp.broadcast_to(shaped, (number, FOOT, 2, FOOT, 2, FOOT, 2))]
    dot_general x11 -> x0, matrix products: 39.9 us -> none  [the longest x2 32.7 us: local(): jnp.dot(deposit, returned, precision=HIGHEST)]
    reduce_sum x7 -> x0, other arithmetic: 33.8 us -> none  [the longest x2 27.7 us: restrict(): return values.reshape(number, FOOT, 2, FOOT, 2, FOOT, 2).mean(axis=(2, 4,...]
  transfers between devices with their start and end apart: 52 -> 0, of which waited for: 15 -> 0; matrix products, arithmetic and copies ran while one was open for 21% -> 0% of each run, Pallas kernels for 0% -> 0%
where the time goes in v1:
time: 118 us
  Pallas kernels  112 us (95%)
  local copies, waits for them, and re-layouts  5.12 us (4%)
    pallas_call x1, Pallas kernels, local(): pl.pallas_call(functools.partial(kernel, (n_x, n_y, n_z, cells)), out_sha...  112 us
    unnamed x7, local copies, waits for them, and re-layouts  3.8 us

profile of v1, /device:TPU:1, one launch (start us, length us, event | category | flops | bytes accessed | tf_op | source)
XLA Modules:
  0.0 118.1 jit_solution(1473011021203722420)
XLA Ops:
  0.6 0.0 copy-start.1
  0.6 0.7 copy-done.1
  1.3 0.7 copy.14.corner
  2.0 112.3 %cycles.1 = (f32[512,128]{1,0:T(8,128)}, f32[1024,128]{1,0:T(8,128)}, f32[1,128]{1,0:T(1,128)}) custom-call(s32[1,4,3]{2,1,0:T(4,128)} %copy.14.corner, s32[1,4]{1,0:T(1,128)} %owner.1, f32[512,128]{1,0:T(8,128)} %bitcast.29, f32[512,128]{1,0:T(8,128)} %bitcast.30, f32[512,128]{1,0:T(8,128)} %bitcast.31, f32[1024,128]{1,0:T(8,128)} %bitcast.26, ...), custom_call_target="tpu_custom_call" | custom-call | tf_op jit(solution)/shard_map/cycles/pallas_call | solution.py:689
  114.3 0.0 copy-start
  114.3 1.3 %slice.3 = f32[1,2]{1,0:T(1,128)} slice(f32[1,128]{1,0:T(1,128)} %get-tuple-element.8), slice={[0:1:1], [0:128:64]} | slice | bytes 16 | tf_op jit(solution)/shard_map/slice | solution.py:764
  115.6 1.7 %copy.18 = f32[16,32,128]{2,1,0:T(8,128)} copy(f32[16,32,128]{2,1,0:T(8,128)} %bitcast.32) | data formatting | bytes 524288
  117.3 0.0 copy-done
  117.3 0.8 copy.19
Async XLA Ops:
  0.6 0.7 copy-start.1
  114.3 3.0 %copy-start = (f32[1024,128]{1,0:T(8,128)S(1)}, f32[1024,128]{1,0:T(8,128)}, u32[]{:S(2)}) copy-start(f32[1024,128]{1,0:T(8,128)} %get-tuple-element.7) | copy-start | bytes 1572868

commit v2 on v1

--- a/solution.py
+++ b/solution.py
@@ -20,6 +20,7 @@
 ROWS = 512
 FROWS = 1024
 SWEEPS = CYCLES * CSWEEPS
+GATHERED = 4
 
 
 def lane_roll(array, shift):
@@ -81,8 +82,11 @@
     code,
     count,
     place_of,
-    flag_out,
-    flag_in,
+    slot_of,
+    flag_of,
+    surf,
+    s_out,
+    s_in,
     d_out,
     d_in,
     r_out,
@@ -93,7 +97,7 @@
     np_in,
     n_send,
     local_sem,
-    flag_sem,
+    s_sem,
     d_send,
     d_recv,
     r_send,
@@ -142,20 +146,23 @@
     places = [
         jnp.where(
             lives[s],
-            ((corner[0, s, 1] >> 5) & 1) * 8 + ((corner[0, s, 2] >> 5) & 7),
+            ((corner[1, 0, s] >> 5) & 1) * 8 + ((corner[2, 0, s] >> 5) & 7),
             -1,
         )
         for s in range(SLOTS)
     ]
     for q in range(members):
         spot = jnp.int32(0)
+        slot = jnp.int32(0)
         flag = jnp.int32(0)
         for s in range(SLOTS):
             mine = owners[s] == q
             spot = jnp.where(mine, places[s], spot)
+            slot = jnp.where(mine, s, slot)
             flag = jnp.where(mine, 1, flag)
         place_of[q] = spot
-        flag_out[q] = jnp.full((1, 128), flag.astype(F32), F32)
+        slot_of[q] = slot
+        flag_of[q] = flag
 
     lane8 = lax.broadcasted_iota(jnp.int32, (8, 128), 1)
     sub8 = lax.broadcasted_iota(jnp.int32, (8, 128), 0)
@@ -165,67 +172,31 @@
 
     zeros = jnp.zeros((32, 128), F32)
 
-    @pl.when(gx == 0)
-    def _():
-        for k in range(SWEEPS):
-            xlo[k] = zeros
-
-    @pl.when(gx == n_x - 1)
-    def _():
-        for k in range(SWEEPS):
-            xhi[k] = zeros
-
-    @pl.when(gy == 0)
-    def _():
-        for k in range(SWEEPS):
-            ylo[k] = zeros[:16]
-
-    @pl.when(gy == n_y - 1)
-    def _():
-        for k in range(SWEEPS):
-            yhi[k] = zeros[:16]
-
-    @pl.when(gz == 0)
-    def _():
-        for k in range(SWEEPS):
-            zlo[k] = zeros[:8]
-
-    @pl.when(gz == n_z - 1)
-    def _():
-        for k in range(SWEEPS):
-            zhi[k] = zeros[:8]
-
-    def halo_copies(k):
-        return (
-            (gx > 0, pot.at[k, pl.ds(0, 32)], xhi.at[k], 0, {"gx": ring(-1)}),
-            (gx < n_x - 1, pot.at[k, pl.ds(ROWS - 32, 32)], xlo.at[k], 1, {"gx": ring(1)}),
-            (gy > 0, yface.at[k, 0], yhi.at[k], 2, {"gy": lax.rem(gy + n_y - 1, n_y)}),
-            (gy < n_y - 1, yface.at[k, 1], ylo.at[k], 3, {"gy": lax.rem(gy + 1, n_y)}),
-            (gz > 0, zface.at[k], zhi.at[k], 4, {"gz": lax.rem(gz + n_z - 1, n_z)}),
-            (gz < n_z - 1, zface.at[k], zlo.at[k], 5, {"gz": lax.rem(gz + 1, n_z)}),
+    def halo(k, sides, act):
+        routes = (
+            (pot.at[k, pl.ds(0, 32)], xhi.at[k], {"gx": ring(-1)}),
+            (pot.at[k, pl.ds(ROWS - 32, 32)], xlo.at[k], {"gx": ring(1)}),
+            (yface.at[k, 0], yhi.at[k], {"gy": lax.rem(gy + n_y - 1, n_y)}),
+            (yface.at[k, 1], ylo.at[k], {"gy": lax.rem(gy + 1, n_y)}),
+            (zface.at[k], zhi.at[k], {"gz": lax.rem(gz + n_z - 1, n_z)}),
+            (zface.at[k], zlo.at[k], {"gz": lax.rem(gz + 1, n_z)}),
         )
-
-    def halo(k, act):
-        for i, (there, src, dst, sem, device) in enumerate(halo_copies(k)):
+        for i in sides:
+            src, dst, device = routes[i]
             copy = pltpu.make_async_remote_copy(
                 src_ref=src,
                 dst_ref=dst,
-                send_sem=h_send.at[k, sem],
-                recv_sem=h_recv.at[k, sem],
+                send_sem=h_send.at[k, i],
+                recv_sem=h_recv.at[k, i],
                 device_id=device,
                 device_id_type=MESH,
             )
-            if act == "recv":
-                there = halo_copies(k)[i ^ 1][0]
-
-            @pl.when(there)
-            def _(copy=copy):
-                if act == "start":
-                    copy.start()
-                elif act == "recv":
-                    copy.wait_recv()
-                else:
-                    copy.wait_send()
+            if act == "start":
+                copy.start()
+            elif act == "recv":
+                copy.wait_recv()
+            else:
+                copy.wait_send()
 
     def faces_of(x, slab, k, acc):
         yface[k, 0, pl.ds(x, 1), :] = slab[0:1]
@@ -236,11 +207,9 @@
             acc = jnp.where(keep, lane_roll(slab[8 * t : 8 * t + 8], 2 * v), acc)
         return acc
 
-    def send_parents(c):
+    def pack_parents(slab_of):
         for x in range(16):
-            slab = pot[c * CSWEEPS, pl.ds(x * 32, 32), :]
-            before = pot[jnp.maximum(c - 1, 0) * CSWEEPS, pl.ds(x * 32, 32), :]
-            slab = jnp.where(c > 0, slab - before, slab)
+            slab = slab_of(x)
             for by in range(2):
                 for y3 in range(2):
                     t = by * 2 + y3
@@ -251,10 +220,13 @@
                 for bz, part in enumerate(group_transpose(parts)):
                     packed[by * 8 + bz, pl.ds(8 * i, 8), :] = part
 
+    def send_parents(c):
+        rows_of = lambda at, x: pot[at, pl.ds(x * 32, 32), :]
+        pack_parents(lambda x: rows_of(c * CSWEEPS + CSWEEPS, x) - rows_of(c * CSWEEPS, x))
         d_in[c, me] = packed[place_of[me]]
 
         def send(i, carry):
-            q = lax.rem(me + i, members)
+            q = lax.rem(me + members - i, members)
             d_out[c, q] = packed[place_of[q]]
             pltpu.make_async_remote_copy(
                 src_ref=d_out.at[c, q],
@@ -268,6 +240,94 @@
 
         lax.fori_loop(1, members, send, 0)
 
+    inner_lane = lambda lane, first: (lane > first) & (lane < first + 15)
+
+    def surface_lane(o):
+        m = o % 32
+        at = jnp.where(m < 16, m, ((m - 16) // 2 + 1) * 16 + (m % 2) * 15)
+        return jnp.where(m < 30, at, -1)
+
+    def stage_surfaces():
+        pack_parents(lambda x: pot[0, pl.ds(x * 32, 32), :])
+        i = lax.broadcasted_iota(jnp.int32, (128, 128), 0)
+        o = lax.broadcasted_iota(jnp.int32, (128, 128), 1)
+        choose = (i == surface_lane(o)).astype(F32)
+        for s in range(SLOTS):
+            block = packed[jnp.maximum(places[s], 0)]
+            odd = (row32 % 2 == 1) & inner_lane(lane32, 0)
+            dense[pl.ds(32 * s, 32), :] = jnp.where(odd, lane_roll(block, 16), block)
+            surf[s, pl.ds(8, 2), :] = block[0:2]
+            surf[s, pl.ds(10, 2), :] = block[30:32]
+        ghost[pl.ds(0, 128), :] = jnp.dot(
+            dense[...], choose, precision=HIGHEST, preferred_element_type=F32
+        )
+        for s in range(SLOTS):
+            block = ghost[pl.ds(32 * s, 32), :]
+            block = jnp.where(lane32 // 32 == row32 % 4, block, 0.0)
+            block = block + pltpu.roll(block, 31, 0)
+            block = block + pltpu.roll(block, 30, 0)
+            dense[pl.ds(32 * s, 32), :] = block
+            surf[s, pl.ds(0, 8), :] = dense[pl.ds(32 * s, 8, stride=4), :]
+
+        def stage(q, carry):
+            slot = slot_of[q]
+            flag = jnp.full((8, 128), flag_of[q].astype(F32), F32)
+            s_out[q, pl.ds(0, 8), :] = jnp.where(lane8 == 31, flag, surf[slot, pl.ds(0, 8), :])
+            s_out[q, pl.ds(8, 4), :] = surf[slot, pl.ds(8, 4), :]
+            return carry
+
+        lax.fori_loop(0, members, stage, 0)
+        s_in[me] = s_out[me]
+
+    def send_surfaces():
+        def send(i, carry):
+            q = lax.rem(me + members - i, members)
+            pltpu.make_async_remote_copy(
+                src_ref=s_out.at[q],
+                dst_ref=s_in.at[me],
+                send_sem=s_sem.at[0],
+                recv_sem=s_sem.at[1],
+                device_id=peer(q),
+                device_id_type=MESH,
+            ).start()
+            return carry
+
+        lax.fori_loop(1, members, send, 0)
+
+    def recv_surfaces():
+        wait_all(s_in, s_sem.at[1])
+        before = jnp.zeros((8, 128), F32)
+        tops = [jnp.zeros((8, 128), F32)] * SLOTS
+        ends = [jnp.zeros((4, 128), F32)] * SLOTS
+        for r in range(members):
+            top = s_in[r, pl.ds(0, 8), :]
+            end = s_in[r, pl.ds(8, 4), :]
+            flag = jnp.sum(jnp.where(lane8 == 31, top, 0.0), axis=1, keepdims=True)
+            flag = jnp.broadcast_to(flag, (8, 128))
+            mark = jnp.where(flag > 0.5, before, -1.0)
+            code[r] = mark
+            before = before + flag
+            for j in range(SLOTS):
+                tops[j] = jnp.where(mark == j, top, tops[j])
+                ends[j] = jnp.where(mark[0:4] == j, end, ends[j])
+        count[...] = before
+        for j in range(SLOTS):
+            for i in range(4):
+                dense[pl.ds(4 * i + j, 8, stride=16), :] = jnp.where(
+                    lane8 // 32 == i, tops[j], 0.0
+                )
+        i = lax.broadcasted_iota(jnp.int32, (128, 128), 0)
+        o = lax.broadcasted_iota(jnp.int32, (128, 128), 1)
+        place = (surface_lane(i) == o).astype(F32)
+        value = jnp.dot(dense[...], place, precision=HIGHEST, preferred_element_type=F32)
+        odd = ((i // 4) % 2 == 1) & inner_lane(o, 112)
+        dense[...] = jnp.where(odd, lane_roll(value, 112), value)
+        for j in range(SLOTS):
+            for y3 in range(2):
+                dense[pl.ds(y3 * 4 + j, 1), :] = ends[j][y3 : y3 + 1]
+                dense[pl.ds(120 + y3 * 4 + j, 1), :] = ends[j][2 + y3 : 3 + y3]
+        spread()
+
     def wait_all(buffer, sem):
         part = buffer.at[pl.ds(0, members - 1)]
         pltpu.make_async_copy(part, part, sem).wait()
@@ -275,20 +335,25 @@
     def recv_parents(c):
         wait_all(d_in.at[c], d_recv.at[c])
 
-        def pick(r, acc):
-            mark = code[r]
+        def pick(r8, acc):
             acc = list(acc)
-            for i in range(4):
-                data = d_in[c, r, pl.ds(8 * i, 8), :]
-                for j in range(SLOTS):
-                    acc[j * 4 + i] = jnp.where(mark == j, data, acc[j * 4 + i])
+            for r in range(GATHERED):
+                r = r8 * GATHERED + r
+                mark = code[r]
+                for i in range(4):
+                    data = d_in[c, r, pl.ds(8 * i, 8), :]
+                    for j in range(SLOTS):
+                        acc[j * 4 + i] = jnp.where(mark == j, data, acc[j * 4 + i])
             return tuple(acc)
 
         blank = jnp.zeros((8, 128), F32)
-        acc = lax.fori_loop(0, members, pick, (blank,) * 16)
+        acc = lax.fori_loop(0, members // GATHERED, pick, (blank,) * 16)
         for j in range(SLOTS):
             for i in range(4):
                 dense[pl.ds(32 * i + j, 8, stride=4), :] = acc[j * 4 + i]
+        spread()
+
+    def spread():
         for y2 in range(2):
             a = jnp.dot(
                 dense[...], expand[:, pl.ds(256 * y2, 128)], precision=HIGHEST,
@@ -395,7 +460,7 @@
             r_in[c, me, pl.ds(8 * i, 8), :] = block_for(me, i)
 
         def send(i, carry):
-            q = lax.rem(me + i, members)
+            q = lax.rem(me + members - i, members)
             for part in range(4):
                 r_out[c, q, pl.ds(8 * part, 8), :] = block_for(q, part)
             pltpu.make_async_remote_copy(
@@ -434,20 +499,30 @@
     first_lane = lane32 == 0
     last_lane = lane32 == 127
 
-    def coarse_sweep(c, s):
-        k = c * CSWEEPS + s
-        halo(k, "recv")
-        beyond = jnp.where(lane8 % 2 == 0, zhi[k], zlo[k])
+    def coarse_sweep(c, k, last):
+        halo(k, range(6), "recv")
+        beyond = jnp.where(
+            lane8 % 2 == 0,
+            jnp.where(gz < n_z - 1, zhi[k], 0.0),
+            jnp.where(gz > 0, zlo[k], 0.0),
+        )
         acc = jnp.zeros((8, 128), F32)
         squares = jnp.zeros((8, 128), F32)
-        follow = jnp.minimum(k + 1, SWEEPS)
-        for x in range(16):
+        for x in [0, 15] + list(range(1, 15)):
             rows = pl.ds(x * 32, 32)
             p = pot[k, rows, :]
-            total = pot[k, pl.ds(x * 32 - 32, 32), :] if x > 0 else xlo[k]
-            total = total + (pot[k, pl.ds(x * 32 + 32, 32), :] if x < 15 else xhi[k])
-            above = jnp.broadcast_to(yhi[k, pl.ds(x, 1), :], (32, 128))
-            below = jnp.broadcast_to(ylo[k, pl.ds(x, 1), :], (32, 128))
+            if x > 0:
+                total = pot[k, pl.ds(x * 32 - 32, 32), :]
+            else:
+                total = jnp.where(gx > 0, xlo[k], 0.0)
+            if x < 15:
+                total = total + pot[k, pl.ds(x * 32 + 32, 32), :]
+            else:
+                total = total + jnp.where(gx < n_x - 1, xhi[k], 0.0)
+            above = jnp.where(gy < n_y - 1, yhi[k, pl.ds(x, 1), :], 0.0)
+            below = jnp.where(gy > 0, ylo[k, pl.ds(x, 1), :], 0.0)
+            above = jnp.broadcast_to(above, (32, 128))
+            below = jnp.broadcast_to(below, (32, 128))
             total = total + jnp.where(row32 == 31, above, pltpu.roll(p, 31, 0))
             total = total + jnp.where(row32 == 0, below, pltpu.roll(p, 1, 0))
             edge = jnp.concatenate(
@@ -455,42 +530,32 @@
             )
             total = total + lane_roll(jnp.where(first_lane, edge, p), -1)
             total = total + lane_roll(jnp.where(last_lane, edge, p), 1)
-            res = comp[rows, :] - diag[rows, :] * p + total
-            sq = res * res
-            squares = squares + ((sq[0:8] + sq[8:16]) + (sq[16:24] + sq[24:32]))
-            new = p + weight[rows, :] * res
+            total = comp[rows, :] + total
+            if last:
+                res = total - diag[rows, :] * p
+                sq = res * res
+                squares = squares + ((sq[0:8] + sq[8:16]) + (sq[16:24] + sq[24:32]))
+                new = p + weight[rows, :] * res
+            else:
+                new = (1.0 - OMEGA) * p + weight[rows, :] * total
             pot[k + 1, rows, :] = new
             acc = faces_of(x, new, k + 1, acc)
+            if x == 15:
+                halo(k + 1, (0, 1), "start")
         zface[k + 1] = acc
-        csum[c] = squares
-
-        @pl.when(k + 1 < SWEEPS)
-        def _():
-            halo(k + 1, "start")
+        halo(k + 1, (2, 3, 4, 5), "start")
+        if last:
+            csum[c] = squares
 
     loads[0].wait()
     acc = jnp.zeros((8, 128), F32)
     for x in range(16):
         acc = faces_of(x, pot[0, pl.ds(x * 32, 32), :], 0, acc)
     zface[0] = acc
+    stage_surfaces()
     pl.semaphore_wait(barrier, members + 1)
-
-    flag_in[me] = flag_out[me]
-
-    def send_flag(i, carry):
-        q = lax.rem(me + i, members)
-        pltpu.make_async_remote_copy(
-            src_ref=flag_out.at[q],
-            dst_ref=flag_in.at[me],
-            send_sem=flag_sem.at[0],
-            recv_sem=flag_sem.at[1],
-            device_id=peer(q),
-            device_id_type=MESH,
-        ).start()
-        return carry
-
-    lax.fori_loop(1, members, send_flag, 0)
-    halo(0, "start")
+    send_surfaces()
+    halo(0, range(6), "start")
 
     rounds = []
     while 2 ** len(rounds) * 2 <= n_x // 2:
@@ -535,13 +600,6 @@
             fweight[rows, :] = OMEGA / d
         for at in (1, 3, 5):
             loads[at].wait()
-        wait_all(flag_in, flag_sem.at[1])
-        before = jnp.zeros((8, 128), F32)
-        for r in range(members):
-            flag = jnp.broadcast_to(flag_in[r], (8, 128))
-            code[r] = jnp.where(flag > 0.5, before, -1.0)
-            before = before + flag
-        count[...] = before
 
     norm_row = lax.broadcasted_iota(jnp.int32, (1, 128), 1)
 
@@ -561,11 +619,8 @@
         n_send[0] = row
         nx_in[gx] = row
 
-        def send(i, carry):
+        for i in sorted(range(1, n_x), key=lambda d: -min(d, n_x - d)):
             norm_copy(n_send.at[0], nx_in.at[gx], 0, {"gx": lax.rem(gx + i, n_x)}).start()
-            return carry
-
-        lax.fori_loop(1, n_x, send, 0)
 
     def turn_norms():
         part = nx_in.at[pl.ds(0, n_x - 1)]
@@ -587,78 +642,70 @@
         row = np_in[0]
         for r in range(1, members):
             row = row + np_in[r]
-        norm_out[...] = jnp.sqrt(row / cells)
+        row = jnp.sqrt(row / cells)
+        for k in range(CYCLES):
+            norm_out[k] = row[0, 64 * k]
 
     def cycle(c, carry):
-        @pl.when(c == CYCLES)
+        use_parents(c)
+        for k in range(CYCLES):
+
+            @pl.when(c == k)
+            def _(k=k):
+                chain_step(2 * k + 1)
+
+        fine_sweeps(c)
+        send_restricted(c)
+        for k in range(CYCLES):
+
+            @pl.when(c == k)
+            def _(k=k):
+                chain_step(2 * k + 2)
+
+        recv_restricted(c)
+
+        def sweep(s, carry):
+            coarse_sweep(c, c * CSWEEPS + s, False)
+            return carry
+
+        lax.fori_loop(0, CSWEEPS - 1, sweep, 0)
+        coarse_sweep(c, c * CSWEEPS + CSWEEPS - 1, True)
+
+        @pl.when(c == CYCLES - 1)
         def _():
             send_norms()
 
         send_parents(c)
-
-        @pl.when(c == 0)
-        def _():
-            prepare()
-
         recv_parents(c)
-
-        @pl.when(c < CYCLES)
-        def _():
-            use_parents(c)
-            for k in range(CYCLES):
-
-                @pl.when(c == k)
-                def _(k=k):
-                    chain_step(2 * k + 1)
-
-            fine_sweeps(c)
-            send_restricted(c)
-            for k in range(CYCLES):
-
-                @pl.when(c == k)
-                def _(k=k):
-                    chain_step(2 * k + 2)
-
-            recv_restricted(c)
-
-            def sweep(s, carry):
-                coarse_sweep(c, s)
-                return carry
-
-            lax.fori_loop(0, CSWEEPS, sweep, 0)
-
         return carry
 
-    lax.fori_loop(0, CYCLES + 1, cycle, 0)
-
-    out_pot = pltpu.make_async_copy(pot.at[SWEEPS], pot_out, local_sem.at[0])
-    out_pot.start()
+    prepare()
+    recv_surfaces()
+    lax.fori_loop(0, CYCLES, cycle, 0)
+
+    pot_out[...] = pot[SWEEPS]
     live = ((row32 % 4).astype(F32) < jnp.concatenate([count[...]] * 4, axis=0)).astype(F32)
     end = CYCLES % 2
     for X in range(32):
         rows = pl.ds(X * 32, 32)
-        fine[1 - end, rows, :] = (fine[end, rows, :] + ghost[pl.ds(X // 2 * 32, 32), :]) * live
-    out_fine = pltpu.make_async_copy(fine.at[1 - end], fine_out, local_sem.at[1])
-    out_fine.start()
+        fine_out[rows, :] = (fine[end, rows, :] + ghost[pl.ds(X // 2 * 32, 32), :]) * live
     turn_norms()
 
-    wait_all(flag_out, flag_sem.at[0])
-    for c in range(CYCLES + 1):
+    wait_all(s_out, s_sem.at[0])
+    for c in range(CYCLES):
         wait_all(d_out.at[c], d_send.at[c])
-    for c in range(CYCLES):
         wait_all(r_out.at[c], r_send.at[c])
+    halo(SWEEPS, range(6), "recv")
 
     def left(k, carry):
-        halo(k, "send")
+        halo(k, range(6), "send")
         return carry
 
-    lax.fori_loop(0, SWEEPS, left, 0)
+    lax.fori_loop(0, SWEEPS + 1, left, 0)
     part = nx_in.at[pl.ds(0, n_x - 1)]
     pltpu.make_async_copy(part, part, n_sem.at[0]).wait()
     end_norms()
     wait_all(np_in, n_sem.at[2])
-    out_pot.wait()
-    out_fine.wait()
 
 
 def local(
@@ -691,22 +738,22 @@
         out_shape=(
             jax.ShapeDtypeStruct((ROWS, 128), F32),
             jax.ShapeDtypeStruct((FROWS, 128), F32),
-            jax.ShapeDtypeStruct((1, 128), F32),
+            jax.ShapeDtypeStruct((CYCLES,), F32),
         ),
         in_specs=[smem, smem] + [hbm] * 6,
-        out_specs=(hbm, hbm, vmem),
+        out_specs=(vmem, vmem, smem),
         scratch_shapes=[
             buf(SWEEPS + 1, ROWS, 128),
             buf(ROWS, 128),
             buf(ROWS, 128),
             buf(ROWS, 128),
             buf(ROWS, 128),
-            buf(SWEEPS, 32, 128),
-            buf(SWEEPS, 32, 128),
-            buf(SWEEPS, 16, 128),
-            buf(SWEEPS, 16, 128),
-            buf(SWEEPS, 8, 128),
-            buf(SWEEPS, 8, 128),
+            buf(SWEEPS + 1, 32, 128),
+            buf(SWEEPS + 1, 32, 128),
+            buf(SWEEPS + 1, 16, 128),
+            buf(SWEEPS + 1, 16, 128),
+            buf(SWEEPS + 1, 8, 128),
+            buf(SWEEPS + 1, 8, 128),
             buf(SWEEPS + 1, 2, 16, 128),
             buf(SWEEPS + 1, 8, 128),
             buf(2, FROWS, 128),
@@ -724,10 +771,13 @@
             buf(members, 8, 128),
             buf(8, 128),
             pltpu.SMEM((members,), jnp.int32),
-            buf(members, 1, 128),
-            buf(members, 1, 128),
-            buf(CYCLES + 1, members, 32, 128),
-            buf(CYCLES + 1, members, 32, 128),
+            pltpu.SMEM((members,), jnp.int32),
+            pltpu.SMEM((members,), jnp.int32),
+            buf(SLOTS, 12, 128),
+            buf(members, 12, 128),
+            buf(members, 12, 128),
+            buf(CYCLES, members, 32, 128),
+            buf(CYCLES, members, 32, 128),
             buf(CYCLES, members, 32, 128),
             buf(CYCLES, members, 32, 128),
             buf(CYCLES, 8, 128),
@@ -737,31 +787,36 @@
             buf(2, 1, 128),
             sems((6,)),
             sems((2,)),
-            sems((CYCLES + 1,)),
-            sems((CYCLES + 1,)),
             sems((CYCLES,)),
             sems((CYCLES,)),
-            sems((SWEEPS, 6)),
-            sems((SWEEPS, 6)),
+            sems((CYCLES,)),
+            sems((CYCLES,)),
+            sems((SWEEPS + 1, 6)),
+            sems((SWEEPS + 1, 6)),
             sems((4,)),
             pltpu.SemaphoreType.REGULAR((4,)),
         ],
         compiler_params=pltpu.CompilerParams(
-            collective_id=0, has_side_effects=True, vmem_limit_bytes=60 * 1000 * 1000
+            collective_id=0, has_side_effects=True, vmem_limit_bytes=30 * 1000 * 1000
         ),
         name="cycles",
     )(
-        box_corner,
+        box_corner.transpose(2, 0, 1),
         box_owner,
-        coarse_source.reshape(ROWS, 128),
-        coarse_shift.reshape(ROWS, 128),
-        coarse_start.reshape(ROWS, 128),
-        fine_rows(fine_source),
-        fine_rows(fine_shift),
-        fine_rows(fine_start),
+        *(
+            pltpu.with_memory_space_constraint(array, pltpu.HBM)
+            for array in (
+                coarse_source.reshape(ROWS, 128),
+                coarse_shift.reshape(ROWS, 128),
+                coarse_start.reshape(ROWS, 128),
+                fine_rows(fine_source),
+                fine_rows(fine_shift),
+                fine_rows(fine_start),
+            )
+        ),
     )
     fine = fine.reshape(256, SLOTS, 128).transpose(1, 0, 2).reshape(SLOTS, 256 * 128)
-    return pot.reshape(coarse_source.shape), fine, norms[0, ::64]
+    return pot.reshape(coarse_source.shape), fine, norms
 
 
 def solution(mesh):

time: 118 us -> 110 us (0.932)
  Pallas kernels: 112 us -> 106 us
  local copies, waits for them, and re-layouts: 5.12 us -> 2.68 us
    pallas_call x1, Pallas kernels: 112 us -> 106 us  [local(): pl.pallas_call(functools.partial(kernel, (n_x, n_y, n_z, cells)), out_sha...]
    slice x1 -> x0, local copies, waits for them, and re-layouts: 1.31 us -> none  [local(): return (pot.reshape(coarse_source.shape), fine, norms[0, ::64])]
where the time goes in v2:
time: 110 us
  Pallas kernels  106 us (96%)
  local copies, waits for them, and re-layouts  2.68 us (2%)
    pallas_call x1, Pallas kernels, local(): pl.pallas_call(functools.partial(kernel, (n_x, n_y, n_z, cells)), out_sha...  106 us
    unnamed x7, local copies, waits for them, and re-layouts  2.68 us

profile of v2, /device:TPU:1, one launch (start us, length us, event | category | flops | bytes accessed | tf_op | source)
XLA Modules:
  0.0 109.7 jit_solution(1303749192917732064)
XLA Ops:
  0.6 0.0 copy-start
  0.6 0.0 copy-start.1
  0.7 0.7 copy-done
  1.3 0.0 copy-done.1
  1.3 106.4 %cycles.1 = (f32[512,128]{1,0:T(8,128)S(1)}, f32[1024,128]{1,0:T(8,128)S(1)}, f32[2]{0:T(128)S(1)}) custom-call(s32[3,1,4]{2,1,0:T(1,128)S(1)} %bitcast.27, s32[1,4]{1,0:T(1,128)S(1)} %copy-done.1, f32[512,128]{1,0:T(8,128)} %bitcast.31, f32[512,128]{1,0:T(8,128)} %bitcast.32, f32[512,128]{1,0:T(8,128)} %bitcast.33, f32[1024,128]{1,0:T(8,128)} %bitcast.28, ...), custom_call_target="tpu_custom_call" | custom-call | tf_op jit(solution)/shard_map/cycles/pallas_call | solution.py:736
  107.7 0.7 copy.18
  108.4 0.8 copy.19
  109.2 0.5 copy.20
Async XLA Ops:
  0.6 0.7 copy-start
  0.6 0.7 copy-start.1

commit v3 on v2

--- a/solution.py
+++ b/solution.py
@@ -21,6 +21,7 @@
 FROWS = 1024
 SWEEPS = CYCLES * CSWEEPS
 GATHERED = 4
+PITCH = 72
 
 
 def lane_roll(array, shift):
@@ -59,6 +60,7 @@
     diag,
     weight,
     comp,
+    beside_sum,
     xlo,
     xhi,
     ylo,
@@ -213,10 +215,10 @@
             for by in range(2):
                 for y3 in range(2):
                     t = by * 2 + y3
-                    mixed[pl.ds(by * 32 + x * 2 + y3, 8, stride=64), :] = slab[8 * t : 8 * t + 8]
+                    mixed[pl.ds(by * 32 + x * 2 + y3, 8, stride=PITCH), :] = slab[8 * t : 8 * t + 8]
         for by in range(2):
             for i in range(4):
-                parts = [mixed[pl.ds(k * 64 + by * 32 + 8 * i, 8), :] for k in range(8)]
+                parts = [mixed[pl.ds(k * PITCH + by * 32 + 8 * i, 8), :] for k in range(8)]
                 for bz, part in enumerate(group_transpose(parts)):
                     packed[by * 8 + bz, pl.ds(8 * i, 8), :] = part
 
@@ -487,50 +489,59 @@
             for i in range(4):
                 parts = [packed[by * 8 + bz, pl.ds(8 * i, 8), :] for bz in range(8)]
                 for k, part in enumerate(group_transpose(parts)):
-                    mixed[pl.ds(k * 64 + by * 32 + 8 * i, 8), :] = part
+                    mixed[pl.ds(k * PITCH + by * 32 + 8 * i, 8), :] = part
         for x in range(16):
             for t in range(4):
                 rows = pl.ds(x * 32 + 8 * t, 8)
                 comp[rows, :] = (
                     source[rows, :]
-                    + mixed[pl.ds(t // 2 * 32 + x * 2 + t % 2, 8, stride=64), :]
+                    + mixed[pl.ds(t // 2 * 32 + x * 2 + t % 2, 8, stride=PITCH), :]
                 )
 
-    first_lane = lane32 == 0
-    last_lane = lane32 == 127
+    edge_lane = (lane8 == 0) | (lane8 == 127)
+
+    def coarse_inner(k):
+        for x in range(16):
+            p = pot[k, pl.ds(x * 32, 32), :]
+            total = jnp.where(row32 < 31, pltpu.roll(p, 31, 0), 0.0)
+            total = total + jnp.where(row32 > 0, pltpu.roll(p, 1, 0), 0.0)
+            total = total + jnp.where(lane32 < 127, lane_roll(p, -1), 0.0)
+            total = total + jnp.where(lane32 > 0, lane_roll(p, 1), 0.0)
+            if x > 0:
+                total = total + pot[k, pl.ds(x * 32 - 32, 32), :]
+            if x < 15:
+                total = total + pot[k, pl.ds(x * 32 + 32, 32), :]
+            beside_sum[pl.ds(x * 32, 32), :] = total
 
     def coarse_sweep(c, k, last):
         halo(k, range(6), "recv")
         beyond = jnp.where(
             lane8 % 2 == 0,
-            jnp.where(gz < n_z - 1, zhi[k], 0.0),
-            jnp.where(gz > 0, zlo[k], 0.0),
+            jnp.where(gz > 0, lane_roll(zlo[k], 1), 0.0),
+            jnp.where(gz < n_z - 1, lane_roll(zhi[k], -1), 0.0),
         )
         acc = jnp.zeros((8, 128), F32)
         squares = jnp.zeros((8, 128), F32)
         for x in [0, 15] + list(range(1, 15)):
             rows = pl.ds(x * 32, 32)
             p = pot[k, rows, :]
-            if x > 0:
-                total = pot[k, pl.ds(x * 32 - 32, 32), :]
-            else:
-                total = jnp.where(gx > 0, xlo[k], 0.0)
-            if x < 15:
-                total = total + pot[k, pl.ds(x * 32 + 32, 32), :]
-            else:
+            total = comp[rows, :] + beside_sum[rows, :]
+            if x == 0:
+                total = total + jnp.where(gx > 0, xlo[k], 0.0)
+            if x == 15:
                 total = total + jnp.where(gx < n_x - 1, xhi[k], 0.0)
             above = jnp.where(gy < n_y - 1, yhi[k, pl.ds(x, 1), :], 0.0)
             below = jnp.where(gy > 0, ylo[k, pl.ds(x, 1), :], 0.0)
-            above = jnp.broadcast_to(above, (32, 128))
-            below = jnp.broadcast_to(below, (32, 128))
-            total = total + jnp.where(row32 == 31, above, pltpu.roll(p, 31, 0))
-            total = total + jnp.where(row32 == 0, below, pltpu.roll(p, 1, 0))
-            edge = jnp.concatenate(
-                [lane_roll(beyond, -2 * (x * 4 + t)) for t in range(4)], axis=0
-            )
-            total = total + lane_roll(jnp.where(first_lane, edge, p), -1)
-            total = total + lane_roll(jnp.where(last_lane, edge, p), 1)
-            total = comp[rows, :] + total
+            parts = []
+            for t in range(4):
+                edge = lane_roll(beyond, -2 * (x * 4 + t))
+                part = total[8 * t : 8 * t + 8] + jnp.where(edge_lane, edge, 0.0)
+                if t == 0:
+                    part = part + jnp.where(sub8 == 0, jnp.broadcast_to(below, (8, 128)), 0.0)
+                if t == 3:
+                    part = part + jnp.where(sub8 == 7, jnp.broadcast_to(above, (8, 128)), 0.0)
+                parts.append(part)
+            total = jnp.concatenate(parts, axis=0)
             if last:
                 res = total - diag[rows, :] * p
                 sq = res * res
@@ -666,6 +677,7 @@
 
         def sweep(s, carry):
             coarse_sweep(c, c * CSWEEPS + s, False)
+            coarse_inner(c * CSWEEPS + s + 1)
             return carry
 
         lax.fori_loop(0, CSWEEPS - 1, sweep, 0)
@@ -676,10 +688,12 @@
             send_norms()
 
         send_parents(c)
+        coarse_inner(c * CSWEEPS + CSWEEPS)
         recv_parents(c)
         return carry
 
     prepare()
+    coarse_inner(0)
     recv_surfaces()
     lax.fori_loop(0, CYCLES, cycle, 0)
 
@@ -744,6 +758,7 @@
         out_specs=(vmem, vmem, smem),
         scratch_shapes=[
             buf(SWEEPS + 1, ROWS, 128),
+            buf(ROWS, 128),
             buf(ROWS, 128),
             buf(ROWS, 128),
             buf(ROWS, 128),
@@ -766,7 +781,7 @@
             buf(ROWS, 128),
             buf(128, 512),
             buf(16, 32, 128),
-            buf(ROWS, 128),
+            buf(8 * PITCH, 128),
             buf(SLOTS, 32, 128),
             buf(members, 8, 128),
             buf(8, 128),

time: 110 us -> 109 us (level)
  no operation moved by 1% of the time
where the time goes in v3:
time: 109 us
  Pallas kernels  105 us (96%)
  local copies, waits for them, and re-layouts  2.68 us (2%)
    pallas_call x1, Pallas kernels, local(): pl.pallas_call(functools.partial(kernel, (n_x, n_y, n_z, cells)), out_sha...  105 us
    unnamed x7, local copies, waits for them, and re-layouts  2.68 us

profile of v3, /device:TPU:1, one launch (start us, length us, event | category | flops | bytes accessed | tf_op | source)
XLA Modules:
  0.0 108.7 jit_solution(9718984248059415284)
XLA Ops:
  0.6 0.0 copy-start
  0.6 0.0 copy-start.1
  0.7 0.7 copy-done
  1.3 0.0 copy-done.1
  1.3 105.4 %cycles.1 = (f32[512,128]{1,0:T(8,128)S(1)}, f32[1024,128]{1,0:T(8,128)S(1)}, f32[2]{0:T(128)S(1)}) custom-call(s32[3,1,4]{2,1,0:T(1,128)S(1)} %bitcast.27, s32[1,4]{1,0:T(1,128)S(1)} %copy-done.1, f32[512,128]{1,0:T(8,128)} %bitcast.31, f32[512,128]{1,0:T(8,128)} %bitcast.32, f32[512,128]{1,0:T(8,128)} %bitcast.33, f32[1024,128]{1,0:T(8,128)} %bitcast.28, ...), custom_call_target="tpu_custom_call" | custom-call | tf_op jit(solution)/shard_map/cycles/pallas_call | solution.py:750
  106.7 0.7 copy.18
  107.4 0.8 copy.19
  108.2 0.5 copy.20
Async XLA Ops:
  0.6 0.7 copy-start
  0.6 0.7 copy-start.1

commit v4 on v3

--- a/solution.py
+++ b/solution.py
@@ -28,24 +28,19 @@
     return pltpu.roll(array, shift % 128, 1)
 
 
-def group_transpose(parts):
-    group = lax.broadcasted_iota(jnp.int32, (8, 128), 1) // 16
-    parts = list(parts)
-    for step in (1, 2, 4):
-        clear = (group & step) == 0
-        for i in range(8):
-            if i & step:
-                continue
-            a, b = parts[i], parts[i + step]
-            parts[i] = jnp.where(clear, a, lane_roll(b, 16 * step))
-            parts[i + step] = jnp.where(clear, lane_roll(a, -16 * step), b)
+def in_parts(value):
+    parts = []
+    for _ in range(3):
+        cut = value.astype(jnp.bfloat16)
+        parts.append(cut)
+        value = value - cut.astype(F32)
     return parts
 
 
 def kernel(
     sizes,
-    corner,
-    owner,
+    corner_hbm,
+    owner_hbm,
     source_hbm,
     shift_hbm,
     start_hbm,
@@ -79,11 +74,16 @@
     ghost,
     wide,
     packed,
+    halves,
+    placed,
+    lane_in,
+    lane_out,
     mixed,
     rblocks,
     code,
     count,
-    place_of,
+    corner,
+    owner,
     slot_of,
     flag_of,
     surf,
@@ -117,6 +117,25 @@
     def peer(q):
         return {"gy": q // n_z, "gz": lax.rem(q, n_z)}
 
+    barrier = pltpu.get_barrier_semaphore()
+
+    def greet(i, carry):
+        q = lax.rem(me + i, members)
+        pl.semaphore_signal(barrier, inc=1, device_id=peer(q), device_id_type=MESH)
+        return carry
+
+    lax.fori_loop(1, members, greet, 0)
+
+    def ring(distance):
+        return lax.rem(gx + distance + n_x, n_x)
+
+    for way in (1, -1):
+        pl.semaphore_signal(barrier, inc=1, device_id={"gx": ring(way)}, device_id_type=MESH)
+
+    tables = [
+        pltpu.make_async_copy(corner_hbm, corner, local_sem.at[6]),
+        pltpu.make_async_copy(owner_hbm, owner, local_sem.at[7]),
+    ]
     loads = [
         pltpu.make_async_copy(start_hbm, pot.at[0], local_sem.at[0]),
         pltpu.make_async_copy(source_hbm, source, local_sem.at[1]),
@@ -125,24 +144,11 @@
         pltpu.make_async_copy(fshift_hbm, fdiag, local_sem.at[4]),
         pltpu.make_async_copy(fstart_hbm, fine.at[0], local_sem.at[5]),
     ]
-    for load in loads:
+    for load in tables + loads:
         load.start()
 
-    barrier = pltpu.get_barrier_semaphore()
-
-    def greet(i, carry):
-        q = lax.rem(me + i, members)
-        pl.semaphore_signal(barrier, inc=1, device_id=peer(q), device_id_type=MESH)
-        return carry
-
-    lax.fori_loop(1, members, greet, 0)
-
-    def ring(distance):
-        return lax.rem(gx + distance + n_x, n_x)
-
-    for way in (1, -1):
-        pl.semaphore_signal(barrier, inc=1, device_id={"gx": ring(way)}, device_id_type=MESH)
-
+    for table in tables:
+        table.wait()
     owners = [owner[0, s] for s in range(SLOTS)]
     lives = [(o >= 0) & (o < members) for o in owners]
     places = [
@@ -153,18 +159,22 @@
         )
         for s in range(SLOTS)
     ]
+    spots = [jnp.maximum(place, 0) for place in places]
     for q in range(members):
-        spot = jnp.int32(0)
         slot = jnp.int32(0)
         flag = jnp.int32(0)
         for s in range(SLOTS):
             mine = owners[s] == q
-            spot = jnp.where(mine, places[s], spot)
             slot = jnp.where(mine, s, slot)
             flag = jnp.where(mine, 1, flag)
-        place_of[q] = spot
         slot_of[q] = slot
         flag_of[q] = flag
+    i = lax.broadcasted_iota(jnp.int32, (384, 128), 0) % 128
+    o = lax.broadcasted_iota(jnp.int32, (384, 128), 1)
+    for s in range(SLOTS):
+        group = spots[s] & 7
+        lane_in[s] = ((i % 16 == o % 16) & (i // 16 == group)).astype(F32).astype(jnp.bfloat16)
+        lane_out[s] = ((i % 16 == o % 16) & (o // 16 == group)).astype(F32).astype(jnp.bfloat16)
 
     lane8 = lax.broadcasted_iota(jnp.int32, (8, 128), 1)
     sub8 = lax.broadcasted_iota(jnp.int32, (8, 128), 0)
@@ -217,19 +227,27 @@
                     t = by * 2 + y3
                     mixed[pl.ds(by * 32 + x * 2 + y3, 8, stride=PITCH), :] = slab[8 * t : 8 * t + 8]
         for by in range(2):
-            for i in range(4):
-                parts = [mixed[pl.ds(k * PITCH + by * 32 + 8 * i, 8), :] for k in range(8)]
-                for bz, part in enumerate(group_transpose(parts)):
-                    packed[by * 8 + bz, pl.ds(8 * i, 8), :] = part
+            for k in range(8):
+                value = mixed[pl.ds(k * PITCH + by * 32, 32), :]
+                for p, part in enumerate(in_parts(value)):
+                    halves[by, pl.ds(k * 32, 32), pl.ds(128 * p, 128)] = part
+        for s in range(SLOTS):
+            rows = jnp.dot(
+                halves[spots[s] >> 3], lane_in[s], preferred_element_type=F32
+            )
+            value = rows[0:32]
+            for k in range(1, 8):
+                value = jnp.where(lane32 // 16 == k, rows[32 * k : 32 * k + 32], value)
+            packed[s] = value
 
     def send_parents(c):
         rows_of = lambda at, x: pot[at, pl.ds(x * 32, 32), :]
         pack_parents(lambda x: rows_of(c * CSWEEPS + CSWEEPS, x) - rows_of(c * CSWEEPS, x))
-        d_in[c, me] = packed[place_of[me]]
+        d_in[c, me] = packed[slot_of[me]]
 
         def send(i, carry):
             q = lax.rem(me + members - i, members)
-            d_out[c, q] = packed[place_of[q]]
+            d_out[c, q] = packed[slot_of[q]]
             pltpu.make_async_remote_copy(
                 src_ref=d_out.at[c, q],
                 dst_ref=d_in.at[c, me],
@@ -255,7 +273,7 @@
         o = lax.broadcasted_iota(jnp.int32, (128, 128), 1)
         choose = (i == surface_lane(o)).astype(F32)
         for s in range(SLOTS):
-            block = packed[jnp.maximum(places[s], 0)]
+            block = packed[s]
             odd = (row32 % 2 == 1) & inner_lane(lane32, 0)
             dense[pl.ds(32 * s, 32), :] = jnp.where(odd, lane_roll(block, 16), block)
             surf[s, pl.ds(8, 2), :] = block[0:2]
@@ -479,17 +497,20 @@
 
     def recv_restricted(c):
         wait_all(r_in.at[c], r_recv.at[c])
-        blocks = [r_in[c, jnp.clip(o, 0, members - 1)] for o in owners]
-        for p in range(16):
-            value = zeros
-            for s in range(SLOTS):
-                value = jnp.where(places[s] == p, blocks[s], value)
-            packed[p] = value
+        for s in range(SLOTS):
+            block = r_in[c, jnp.clip(owners[s], 0, members - 1)]
+            for k in range(8):
+                value = jnp.where(lane32 // 16 == k, block, 0.0)
+                for p, part in enumerate(in_parts(value)):
+                    halves[s % 2, pl.ds(k * 32, 32), pl.ds(128 * p, 128)] = part
+            placed[s] = jnp.dot(halves[s % 2], lane_out[s], preferred_element_type=F32)
         for by in range(2):
-            for i in range(4):
-                parts = [packed[by * 8 + bz, pl.ds(8 * i, 8), :] for bz in range(8)]
-                for k, part in enumerate(group_transpose(parts)):
-                    mixed[pl.ds(k * PITCH + by * 32 + 8 * i, 8), :] = part
+            for k in range(8):
+                value = zeros
+                for s in range(SLOTS):
+                    here = lives[s] & (spots[s] >> 3 == by)
+                    value = value + jnp.where(here, placed[s, pl.ds(32 * k, 32), :], 0.0)
+                mixed[pl.ds(k * PITCH + by * 32, 32), :] = value
         for x in range(16):
             for t in range(4):
                 rows = pl.ds(x * 32 + 8 * t, 8)
@@ -754,7 +775,7 @@
             jax.ShapeDtypeStruct((FROWS, 128), F32),
             jax.ShapeDtypeStruct((CYCLES,), F32),
         ),
-        in_specs=[smem, smem] + [hbm] * 6,
+        in_specs=[hbm] * 8,
         out_specs=(vmem, vmem, smem),
         scratch_shapes=[
             buf(SWEEPS + 1, ROWS, 128),
@@ -780,12 +801,17 @@
             buf(128, 128),
             buf(ROWS, 128),
             buf(128, 512),
-            buf(16, 32, 128),
+            buf(SLOTS, 32, 128),
+            pltpu.VMEM((2, 256, 384), jnp.bfloat16),
+            buf(SLOTS, 256, 128),
+            pltpu.VMEM((SLOTS, 384, 128), jnp.bfloat16),
+            pltpu.VMEM((SLOTS, 384, 128), jnp.bfloat16),
             buf(8 * PITCH, 128),
             buf(SLOTS, 32, 128),
             buf(members, 8, 128),
             buf(8, 128),
-            pltpu.SMEM((members,), jnp.int32),
+            pltpu.SMEM((3, 1, SLOTS), jnp.int32),
+            pltpu.SMEM((1, SLOTS), jnp.int32),
             pltpu.SMEM((members,), jnp.int32),
             pltpu.SMEM((members,), jnp.int32),
             buf(SLOTS, 12, 128),
@@ -800,7 +826,7 @@
             buf(n_x, 1, 128),
             buf(members, 1, 128),
             buf(2, 1, 128),
-            sems((6,)),
+            sems((8,)),
             sems((2,)),
             sems((CYCLES,)),
             sems((CYCLES,)),
@@ -816,11 +842,11 @@
         ),
         name="cycles",
     )(
-        box_corner.transpose(2, 0, 1),
-        box_owner,
         *(
             pltpu.with_memory_space_constraint(array, pltpu.HBM)
             for array in (
+                box_corner.transpose(2, 0, 1),
+                box_owner,
                 coarse_source.reshape(ROWS, 128),
                 coarse_shift.reshape(ROWS, 128),
                 coarse_start.reshape(ROWS, 128),

time: 109 us -> 108 us (level)
    unnamed x7 -> x3, local copies, waits for them, and re-layouts: 2.68 us -> 2.01 us
where the time goes in v4:
time: 108 us
  Pallas kernels  105 us (97%)
  local copies, waits for them, and re-layouts  2.01 us (2%)
    pallas_call x1, Pallas kernels, local(): pl.pallas_call(functools.partial(kernel, (n_x, n_y, n_z, cells)), out_sha...  105 us

profile of v4, /device:TPU:1, one launch (start us, length us, event | category | flops | bytes accessed | tf_op | source)
XLA Modules:
  0.0 107.8 jit_solution(17866297060101278361)
XLA Ops:
  0.6 105.2 %cycles.1 = (f32[512,128]{1,0:T(8,128)S(1)}, f32[1024,128]{1,0:T(8,128)S(1)}, f32[2]{0:T(128)S(1)}) custom-call(s32[3,1,4]{2,1,0:T(1,128)} %bitcast.33, s32[1,4]{1,0:T(1,128)} %owner_hbm.1, f32[512,128]{1,0:T(8,128)} %bitcast.30, f32[512,128]{1,0:T(8,128)} %bitcast.31, f32[512,128]{1,0:T(8,128)} %bitcast.32, f32[1024,128]{1,0:T(8,128)} %bitcast.27, ...), custom_call_target="tpu_custom_call" | custom-call | tf_op jit(solution)/shard_map/cycles/pallas_call | solution.py:771
  105.8 0.7 copy.18
  106.5 0.8 copy.19
  107.3 0.5 copy.20

commit v5 on v4

--- a/solution.py
+++ b/solution.py
@@ -26,6 +26,24 @@
 
 def lane_roll(array, shift):
     return pltpu.roll(array, shift % 128, 1)
+
+
+def far_first(n_y, n_z):
+    def hops(offset):
+        return min(offset[0], n_y // 2 - offset[0]) + min(offset[2], n_z - offset[2])
+
+    def link(offset):
+        dy, _, dz = offset
+        return (0, dz <= n_z // 2) if dz else (1, dy <= n_y // 4) if dy else (2, True)
+
+    queues = {}
+    every = [(y, c, z) for y in range(n_y // 2) for c in range(2) for z in range(n_z)][1:]
+    for offset in sorted(every, key=lambda o: -hops(o)):
+        queues.setdefault(link(offset), []).append(offset)
+    order = []
+    while any(queues.values()):
+        order += [queue.pop(0) for queue in queues.values() if queue]
+    return order
 
 
 def in_parts(value):
@@ -114,6 +132,11 @@
     gx, gy, gz = lax.axis_index("gx"), lax.axis_index("gy"), lax.axis_index("gz")
     me = gy * n_z + gz
 
+    def others():
+        for dy, dc, dz in far_first(n_y, n_z):
+            y = lax.rem(gy // 2 + dy, n_y // 2) * 2 + lax.rem(gy + dc, 2)
+            yield y * n_z + lax.rem(gz + dz, n_z)
+
     def peer(q):
         return {"gy": q // n_z, "gz": lax.rem(q, n_z)}
 
@@ -245,8 +268,7 @@
         pack_parents(lambda x: rows_of(c * CSWEEPS + CSWEEPS, x) - rows_of(c * CSWEEPS, x))
         d_in[c, me] = packed[slot_of[me]]
 
-        def send(i, carry):
-            q = lax.rem(me + members - i, members)
+        def send(q):
             d_out[c, q] = packed[slot_of[q]]
             pltpu.make_async_remote_copy(
                 src_ref=d_out.at[c, q],
@@ -256,9 +278,9 @@
                 device_id=peer(q),
                 device_id_type=MESH,
             ).start()
-            return carry
-
-        lax.fori_loop(1, members, send, 0)
+
+        for q in others():
+            send(q)
 
     inner_lane = lambda lane, first: (lane > first) & (lane < first + 15)
 
@@ -300,8 +322,7 @@
         s_in[me] = s_out[me]
 
     def send_surfaces():
-        def send(i, carry):
-            q = lax.rem(me + members - i, members)
+        def send(q):
             pltpu.make_async_remote_copy(
                 src_ref=s_out.at[q],
                 dst_ref=s_in.at[me],
@@ -310,9 +331,9 @@
                 device_id=peer(q),
                 device_id_type=MESH,
             ).start()
-            return carry
-
-        lax.fori_loop(1, members, send, 0)
+
+        for q in others():
+            send(q)
 
     def recv_surfaces():
         wait_all(s_in, s_sem.at[1])
@@ -479,8 +500,7 @@
         for i in range(4):
             r_in[c, me, pl.ds(8 * i, 8), :] = block_for(me, i)
 
-        def send(i, carry):
-            q = lax.rem(me + members - i, members)
+        def send(q):
             for part in range(4):
                 r_out[c, q, pl.ds(8 * part, 8), :] = block_for(q, part)
             pltpu.make_async_remote_copy(
@@ -491,9 +511,9 @@
                 device_id=peer(q),
                 device_id_type=MESH,
             ).start()
-            return carry
-
-        lax.fori_loop(1, members, send, 0)
+
+        for q in others():
+            send(q)
 
     def recv_restricted(c):
         wait_all(r_in.at[c], r_recv.at[c])
@@ -663,11 +683,11 @@
         n_send[1] = row
         np_in[me] = row
 
-        def send(i, carry):
-            norm_copy(n_send.at[1], np_in.at[me], 2, peer(lax.rem(me + i, members))).start()
-            return carry
-
-        lax.fori_loop(1, members, send, 0)
+        def send(q):
+            norm_copy(n_send.at[1], np_in.at[me], 2, peer(q)).start()
+
+        for q in others():
+            send(q)
 
     def end_norms():
         wait_all(np_in, n_sem.at[3])

time: 108 us -> 106 us (0.981)
  Pallas kernels: 105 us -> 103 us
    pallas_call x1, Pallas kernels: 105 us -> 103 us  [local(): pl.pallas_call(functools.partial(kernel, (n_x, n_y, n_z, cells)), out_sha...]
where the time goes in v5:
time: 106 us
  Pallas kernels  103 us (97%)
  local copies, waits for them, and re-layouts  2.01 us (2%)
    pallas_call x1, Pallas kernels, local(): pl.pallas_call(functools.partial(kernel, (n_x, n_y, n_z, cells)), out_sha...  103 us

profile of v5, /device:TPU:1, one launch (start us, length us, event | category | flops | bytes accessed | tf_op | source)
XLA Modules:
  0.0 105.5 jit_solution(15267290707242493857)
XLA Ops:
  0.6 102.9 %cycles.1 = (f32[512,128]{1,0:T(8,128)S(1)}, f32[1024,128]{1,0:T(8,128)S(1)}, f32[2]{0:T(128)S(1)}) custom-call(s32[3,1,4]{2,1,0:T(1,128)} %bitcast.33, s32[1,4]{1,0:T(1,128)} %owner_hbm.1, f32[512,128]{1,0:T(8,128)} %bitcast.30, f32[512,128]{1,0:T(8,128)} %bitcast.31, f32[512,128]{1,0:T(8,128)} %bitcast.32, f32[1024,128]{1,0:T(8,128)} %bitcast.27, ...), custom_call_target="tpu_custom_call" | custom-call | tf_op jit(solution)/shard_map/cycles/pallas_call | solution.py:791
  103.5 0.7 copy.18
  104.2 0.8 copy.19
  105.0 0.5 copy.20
